TPU v7x, 8 devices: a whole 2x2x1 slice. The times are simulated.
8 devices in a mesh: rep: 1 (over z), dp: 8 (over x, y, core).
Axes of the slice: x: 2, y: 2, z: 1, core: 2. Of those that a mesh axis runs over, the one named last changes fastest.
Arguments:
- x: bfloat16 [8, 2048, 1280], P(('rep', 'dp'))
- dy: bfloat16 [8, 2048, 1280], P(('rep', 'dp'))
- w_gate: bfloat16 [2, 1280, 5120], P(None, 'dp')
- w_up: bfloat16 [2, 1280, 5120], P(None, 'dp')
- w_down: bfloat16 [2, 5120, 1280], P(None, 'dp')
- m_w_gate: float32 [2, 1280, 5120], P(None, 'dp')
- m_w_up: float32 [2, 1280, 5120], P(None, 'dp')
- m_w_down: float32 [2, 5120, 1280], P(None, 'dp')
- v_w_gate: float32 [2, 1280, 5120], P(None, 'dp')
- v_w_up: float32 [2, 1280, 5120], P(None, 'dp')
- v_w_down: float32 [2, 5120, 1280], P(None, 'dp')
Outputs:
- output 1: bfloat16 [2, 1280, 5120], P('rep', 'dp')
- output 2: bfloat16 [2, 1280, 5120], P('rep', 'dp')
- output 3: bfloat16 [2, 5120, 1280], P('rep', 'dp')
- output 4: float32 [2, 1280, 5120], P('rep', 'dp')
- output 5: float32 [2, 1280, 5120], P('rep', 'dp')
- output 6: float32 [2, 5120, 1280], P('rep', 'dp')
- output 7: float32 [2, 1280, 5120], P('rep', 'dp')
- output 8: float32 [2, 1280, 5120], P('rep', 'dp')
- output 9: float32 [2, 5120, 1280], P('rep', 'dp')
All inputs are finite; a program needn't handle non-finite values.
Results may differ from a plain program's by a relative error of at most 0.022.
Values are sent between devices in bfloat16 or wider.
A program may use at most 2 GiB of HBM per device.

v0:
```python
import jax
import jax.numpy as jnp
from jax import lax
from jax.sharding import PartitionSpec as P

NAMES = ("w_gate", "w_up", "w_down")


def matmul(a, w):
    return jnp.dot(a, w, preferred_element_type=jnp.float32).astype(jnp.bfloat16)


def normed(h):
    wide = h.astype(jnp.float32)
    scale = lax.rsqrt(jnp.mean(wide**2, -1, keepdims=True) + 1e-6)
    return (wide * scale).astype(jnp.bfloat16)


def layer(h, w):
    a = normed(h)
    gate = jnp.dot(a, w["w_gate"], preferred_element_type=jnp.float32)
    up = jnp.dot(a, w["w_up"], preferred_element_type=jnp.float32)
    return h + matmul((jax.nn.silu(gate) * up).astype(jnp.bfloat16), w["w_down"])


def adamw(w, m, v, g):
    m = 0.9 * m + 0.1 * g
    v = 0.95 * v + 0.05 * g * g
    step = m * lax.rsqrt(v + 1e-8) + 0.1 * w
    return (w - 0.02 * step).astype(jnp.bfloat16), m, v


def clipped(gradients, sum_of_squares, count):
    factor = jnp.minimum(1.0, 0.5 * lax.rsqrt(sum_of_squares / count + 1e-30))
    return [g * factor for g in gradients]


def solution(mesh):
    def fetched(weights, number):
        return {name: lax.all_gather(w[number], "dp", axis=0, tiled=True) for name, w in zip(NAMES, weights, strict=True)}

    def step(x, dy, *arrays):
        weights, m, v = (arrays[i : i + 3] for i in (0, 3, 6))
        layers = weights[0].shape[0]
        h, kept = x[0], []
        for number in range(layers):
            kept.append(h)
            h = layer(h, fetched(weights, number))
        by_h, mine = dy[0], [None] * layers
        for number in reversed(range(layers)):
            _, back = jax.vjp(lambda w, h: layer(h, w), fetched(weights, number), kept[number])
            by_w, by_h = back(by_h)
            mine[number] = [lax.psum_scatter(by_w[name], "dp", scatter_dimension=0, tiled=True) for name in NAMES]
        gradients = [jnp.stack([mine[number][i] for number in range(layers)]).astype(jnp.float32) for i in range(3)]
        squares = lax.psum(sum(jnp.sum(g * g) for g in gradients), "dp")
        gradients = clipped(gradients, squares, lax.psum(1, "dp") * sum(g.size for g in gradients))
        new = [adamw(w.astype(jnp.float32), m, v, g) for w, m, v, g in zip(weights, m, v, gradients, strict=True)]
        return tuple(one[which] for which in range(3) for one in new)

    states, cut = P(("rep", "dp"), None, None), P(None, "dp", None)
    return jax.shard_map(
        step,
        mesh=mesh,
        in_specs=(states, states) + (cut,) * 9,
        out_specs=(P("rep", "dp", None),) * 9,
        check_vma=False,
    )
```

profile of v0, /device:TPU:0, one launch (start us, length us, event | category | flops | bytes accessed | tf_op | source)
XLA Modules:
  0.0 1218.1 jit_solution(15541939812175594379)
XLA Ops:
  7.2 3.8 fusion.105
  11.1 0.0 all-gather.15.cloned.1.call-start
  11.1 4.0 fusion.104
  15.2 0.0 all-gather.17.cloned.1.call-start
  15.2 1.9 fusion.103
  17.2 0.5 all-gather.21.cloned.1.call-update
  17.8 0.5 all-gather.23.cloned.1.call-update
  18.4 0.5 all-gather.19.cloned.1.call-update
  18.9 7.9 copy.20
  26.8 3.6 fusion.36
  30.4 7.9 copy.21
  38.3 44.3 %all-gather.13.cloned.1.call-done = bf16[1,1280,5120]{2,1,0:T(8,128)(2,1)} async-done(((bf16[1,160,5120]{2,1,0:T(8,128)(2,1)}), bf16[1,1280,5120]{2,1,0:T(8,128)(2,1)}) %all-gather.13.cloned.1.call-update) | async-done | bytes 13107216 | tf_op jit(solution)/shard_map/all_gather | solution.py:40
  82.6 35.1 %fusion.34 = f32[2048,5120]{1,0:T(8,128)} fusion(bf16[1,1280,5120]{2,1,0:T(8,128)(2,1)} %all-gather.13.cloned.1.call-done, bf16[1,2048,1280]{1,2,0:T(8,128)(2,1)} %copy.20, f32[2048]{0:T(1024)S(1)} %add_rsqrt_fusion), kind=kOutput, calls=%fused_computation.49 | convolution fusion | flops 26851409920 | bytes 60301312 | tf_op jit(solution)/shard_map/dot_general | solution.py:21
  117.7 35.9 %all-gather.15.cloned.1.call-done = bf16[1,1280,5120]{2,1,0:T(8,128)(2,1)} async-done(((bf16[1,160,5120]{2,1,0:T(8,128)(2,1)}), bf16[1,1280,5120]{2,1,0:T(8,128)(2,1)}) %all-gather.15.cloned.1.call-update) | async-done | bytes 13107216 | tf_op jit(solution)/shard_map/all_gather | solution.py:40
  153.5 51.8 %multiply_convert_fusion.1 = (bf16[2048,5120]{1,0:T(8,128)(2,1)}, f32[2048,5120]{1,0:T(8,128)}) fusion(f32[2048,5120]{1,0:T(8,128)} %fusion.34, bf16[1,1280,5120]{2,1,0:T(8,128)(2,1)} %all-gather.15.cloned.1.call-done, bf16[1,2048,1280]{1,2,0:T(8,128)(2,1)} %copy.20, f32[2048]{0:T(1024)S(1)} %add_rsqrt_fusion), kind=kOutput, calls=%fused_computation.17 | convolution fusion | flops 26914324480 | bytes 123215872 | tf_op jit(solution)/shard_map/dot_general | solution.py:22
  205.4 19.1 %all-gather.17.cloned.1.call-done = bf16[1,5120,1280]{2,1,0:T(8,128)(2,1)} async-done(((bf16[1,640,1280]{2,1,0:T(8,128)(2,1)}), bf16[1,5120,1280]{2,1,0:T(8,128)(2,1)}) %all-gather.17.cloned.1.call-update) | async-done | bytes 13107216 | tf_op jit(solution)/shard_map/all_gather | solution.py:40
  224.5 48.5 %fusion.40 = (f32[2048]{0:T(1024)S(1)}, bf16[2048,1280]{0,1:T(8,128)(2,1)}) fusion(bf16[2048,5120]{1,0:T(8,128)(2,1)} %get-tuple-element.24, bf16[1,5120,1280]{2,1,0:T(8,128)(2,1)} %all-gather.17.cloned.1.call-done, bf16[1,2048,1280]{1,2,0:T(8,128)(2,1)} %copy.20), kind=kOutput, calls=%fused_computation.58 | convolution fusion | flops 26856650752 | bytes 44572672 | tf_op jit(solution)/shard_map/dot_general | solution.py:10
  273.0 22.3 %all-gather.21.cloned.1.call-done = bf16[1,5120,1280]{2,1,0:T(8,128)(2,1)} async-done(((bf16[1,640,1280]{2,1,0:T(8,128)(2,1)}), bf16[1,5120,1280]{2,1,0:T(8,128)(2,1)}) %all-gather.21.cloned.1.call-update) | async-done | bytes 13107216 | tf_op jit(solution)/shard_map/all_gather | solution.py:40
  295.3 34.2 %convolution_convert_fusion.1 = bf16[2048,5120]{1,0:T(8,128)(2,1)} fusion(bf16[1,5120,1280]{2,1,0:T(8,128)(2,1)} %all-gather.21.cloned.1.call-done, bf16[1,2048,1280]{2,1,0:T(8,128)(2,1)} %param.12), kind=kOutput, calls=%fused_computation.29 | convolution fusion | flops 26854031360 | bytes 39321600 | tf_op jit(solution)/shard_map/transpose(jvp())/dot_general | solution.py:10
  329.5 36.6 %all-gather.23.cloned.1.call-done = bf16[1,1280,5120]{2,1,0:T(8,128)(2,1)} async-done(((bf16[1,160,5120]{2,1,0:T(8,128)(2,1)}), bf16[1,1280,5120]{2,1,0:T(8,128)(2,1)}) %all-gather.23.cloned.1.call-update) | async-done | bytes 13107216 | tf_op jit(solution)/shard_map/all_gather | solution.py:40
  366.1 35.1 %fusion.21 = f32[2048,5120]{1,0:T(8,128)} fusion(bf16[1,1280,5120]{2,1,0:T(8,128)(2,1)} %all-gather.23.cloned.1.call-done, bf16[2048,1280]{0,1:T(8,128)(2,1)} %get-tuple-element.27, f32[2048]{0:T(1024)S(1)} %fusion.91), kind=kOutput, calls=%fused_computation.36 | convolution fusion | flops 26851409920 | bytes 60301312 | tf_op jit(solution)/shard_map/jvp()/dot_general | solution.py:22
  401.2 35.7 %all-gather.19.cloned.1.call-done = bf16[1,1280,5120]{2,1,0:T(8,128)(2,1)} async-done(((bf16[1,160,5120]{2,1,0:T(8,128)(2,1)}), bf16[1,1280,5120]{2,1,0:T(8,128)(2,1)}) %all-gather.19.cloned.1.call-update) | async-done | bytes 13107216 | tf_op jit(solution)/shard_map/all_gather | solution.py:40
  436.9 59.3 %fusion.2 = (bf16[2048,5120]{1,0:T(8,128)(2,1)}, f32[2048,5120]{1,0:T(8,128)}) fusion(f32[2048,5120]{1,0:T(8,128)} %fusion.21, bf16[2048,5120]{1,0:T(8,128)(2,1)} %convolution_convert_fusion.1, bf16[1,1280,5120]{2,1,0:T(8,128)(2,1)} %all-gather.19.cloned.1.call-done, bf16[2048,1280]{0,1:T(8,128)(2,1)} %get-tuple-element.27, f32[2048]{0:T(1024)S(1)} %fusion.91), kind=kOutput, calls=%fused_computation.8 | convolution fusion | flops 26977239040 | bytes 144187392 | tf_op jit(solution)/shard_map/jvp()/dot_general | solution.py:21
  496.2 35.7 %fusion.49 = bf16[2048,1280]{0,1:T(8,128)(2,1)} fusion(bf16[2048,5120]{1,0:T(8,128)(2,1)} %get-tuple-element.28, bf16[1,1280,5120]{2,1,0:T(8,128)(2,1)} %all-gather.19.cloned.1.call-done), kind=kOutput, calls=%fused_computation.80 | convolution fusion | flops 26843545600 | bytes 39321600 | tf_op jit(solution)/shard_map/transpose(jvp())/dot_general | solution.py:21
  531.9 41.0 %fusion.42 = (f32[2048]{0:T(1024)S(1)}, bf16[2048,1280]{0,1:T(8,128)(2,1)}) fusion(bf16[2048,1280]{0,1:T(8,128)(2,1)S(1)} %copy-done.8, bf16[2048,1280]{0,1:T(8,128)(2,1)} %fusion.49, bf16[1,1280,5120]{2,1,0:T(8,128)(2,1)} %all-gather.23.cloned.1.call-done, bf16[2048,5120]{1,0:T(8,128)(2,1)} %convolution_convert_fusion.1, f32[2048,5120]{1,0:T(8,128)} %get-tuple-element.29), kind=kOutput, calls=%fused_computation.60 | convolution fusion | flops 26922186752 | bytes 91758592 | tf_op jit(solution)/shard_map/transpose(jvp())/dot_general | solution.py:22
  572.9 12.4 %fusion.80 = bf16[2048,1280]{0,1:T(8,128)(2,1)} fusion(bf16[2048,1280]{0,1:T(8,128)(2,1)} %get-tuple-element.27, bf16[2048,1280]{0,1:T(8,128)(2,1)} %get-tuple-element.31, bf16[1,2048,1280]{1,2,0:T(8,128)(2,1)} %copy.21, f32[2048]{0:T(1024)S(1)} %multiply_multiply_fusion.3, f32[2048]{0:T(1024)S(1)} %copy-done.10), kind=kLoop, calls=%fused_computation.102 | loop fusion | flops 18350080 | bytes 20987904 | tf_op jit(solution)/shard_map/transpose(jvp())/add_any | solution.py:14
  585.3 33.8 %convolution_convert_fusion.2 = bf16[5120,1280]{1,0:T(8,128)(2,1)} fusion(bf16[2048,5120]{1,0:T(8,128)(2,1)} %get-tuple-element.24, bf16[2048,1280]{0,1:T(8,128)(2,1)} %fusion.80), kind=kOutput, calls=%fused_computation.30 | convolution fusion | flops 26850099200 | bytes 39321600 | tf_op jit(solution)/shard_map/transpose(jvp())/dot_general | solution.py:10
  619.1 0.0 reduce-scatter.17.cloned.1.call-start
  619.1 41.9 %fusion.15 = bf16[5120,1280]{1,0:T(8,128)(2,1)} fusion(f32[2048,5120]{1,0:T(8,128)} %fusion.21, bf16[1,2048,1280]{2,1,0:T(8,128)(2,1)} %param.12, f32[2048,5120]{1,0:T(8,128)} %get-tuple-element.29), kind=kOutput, calls=%fused_computation.24 | convolution fusion | flops 26913013760 | bytes 102236160 | tf_op jit(solution)/shard_map/transpose(jvp())/dot_general | solution.py:10
  661.1 35.1 %convolution_convert_fusion = bf16[2048,5120]{1,0:T(8,128)(2,1)} fusion(bf16[2048,1280]{0,1:T(8,128)(2,1)} %fusion.80, bf16[1,5120,1280]{2,1,0:T(8,128)(2,1)} %all-gather.17.cloned.1.call-done), kind=kOutput, calls=%fused_computation.28 | convolution fusion | flops 26854031360 | bytes 39321600 | tf_op jit(solution)/shard_map/transpose(jvp())/dot_general | solution.py:10
  696.2 38.1 %fusion.20 = bf16[1280,5120]{1,0:T(8,128)(2,1)} fusion(bf16[2048,5120]{1,0:T(8,128)(2,1)} %convolution_convert_fusion, f32[2048,5120]{1,0:T(8,128)} %fusion.34, bf16[1,2048,1280]{1,2,0:T(8,128)(2,1)} %copy.20, f32[2048]{0:T(1024)S(1)} %copy-done.15), kind=kOutput, calls=%fused_computation.27 | convolution fusion | flops 26920878080 | bytes 81272832 | tf_op jit(solution)/shard_map/transpose(jvp())/dot_general | solution.py:22
  734.4 0.6 copy-done.11
  735.0 38.1 %fusion.16 = bf16[1280,5120]{1,0:T(8,128)(2,1)} fusion(bf16[2048,5120]{1,0:T(8,128)(2,1)} %convolution_convert_fusion.1, bf16[2048,1280]{0,1:T(8,128)(2,1)} %get-tuple-element.27, f32[2048]{0:T(1024)S(1)} %copy-done.11, f32[2048,5120]{1,0:T(8,128)} %get-tuple-element.29), kind=kOutput, calls=%fused_computation.25 | convolution fusion | flops 26920878080 | bytes 81272832 | tf_op jit(solution)/shard_map/transpose(jvp())/dot_general | solution.py:22
  773.2 48.2 %fusion.17 = bf16[1280,5120]{1,0:T(8,128)(2,1)} fusion(f32[2048,5120]{1,0:T(8,128)} %fusion.34, f32[2048,5120]{1,0:T(8,128)} %get-tuple-element.25, bf16[2048,5120]{1,0:T(8,128)(2,1)} %convolution_convert_fusion, bf16[1,2048,1280]{1,2,0:T(8,128)(2,1)} %copy.20, f32[2048]{0:T(1024)S(1)} %copy-done.15), kind=kOutput, calls=%fused_computation.26 | convolution fusion | flops 26973306880 | bytes 123215872 | tf_op jit(solution)/shard_map/transpose(jvp())/dot_general | solution.py:21
  821.4 0.0 reduce-scatter.9.cloned.1.call-start
  821.4 33.8 %convolution_convert_fusion.3 = bf16[1280,5120]{1,0:T(8,128)(2,1)} fusion(bf16[2048,5120]{1,0:T(8,128)(2,1)} %get-tuple-element.28, bf16[2048,1280]{0,1:T(8,128)(2,1)} %get-tuple-element.27, f32[2048]{0:T(1024)S(1)} %copy-done.11), kind=kOutput, calls=%fused_computation.31 | convolution fusion | flops 26851409920 | bytes 39329792 | tf_op jit(solution)/shard_map/transpose(jvp())/dot_general | solution.py:21
  855.4 4.4 fusion.64
  859.7 21.1 %reduce-scatter.11.cloned.1.call-done = bf16[160,5120]{1,0:T(8,128)(2,1)} async-done(((bf16[1280,5120]{1,0:T(8,128)(2,1)}), bf16[160,5120]{1,0:T(8,128)(2,1)}) %reduce-scatter.11.cloned.1.call-update) | async-done | bytes 1638416 | tf_op jit(solution)/shard_map/reduce_scatter | solution.py:53
  880.8 88.2 %reduce-scatter.13.cloned.1.call-done = bf16[160,5120]{1,0:T(8,128)(2,1)} async-done(((bf16[1280,5120]{1,0:T(8,128)(2,1)}), bf16[160,5120]{1,0:T(8,128)(2,1)}) %reduce-scatter.13.cloned.1.call-update) | async-done | bytes 1638416 | tf_op jit(solution)/shard_map/reduce_scatter | solution.py:53
  969.1 4.2 fusion.63
  973.3 84.2 %reduce-scatter.7.cloned.1.call-done = bf16[160,5120]{1,0:T(8,128)(2,1)} async-done(((bf16[1280,5120]{1,0:T(8,128)(2,1)}), bf16[160,5120]{1,0:T(8,128)(2,1)}) %reduce-scatter.7.cloned.1.call-update) | async-done | bytes 1638416 | tf_op jit(solution)/shard_map/reduce_scatter | solution.py:53
  1057.5 88.2 %reduce-scatter.9.cloned.1.call-done = bf16[160,5120]{1,0:T(8,128)(2,1)} async-done(((bf16[1280,5120]{1,0:T(8,128)(2,1)}), bf16[160,5120]{1,0:T(8,128)(2,1)}) %reduce-scatter.9.cloned.1.call-update) | async-done | bytes 1638416 | tf_op jit(solution)/shard_map/reduce_scatter | solution.py:53
  1145.7 4.2 fusion.62
  1151.9 22.6 %psum.7 = f32[]{:T(128)} all-reduce(f32[]{:T(128)S(6)} %add.99), channel_id=1, replica_groups=mesh['rep'=1,'dp'=8] {'dp'}, use_global_device_ids=true, to_apply=%region_12.13 | all-reduce | flops 1 | bytes 8 | tf_op jit(solution)/shard_map/psum | solution.py:55
  1175.2 13.5 %fusion.70 = (bf16[2,640,1280]{2,1,0:T(8,128)(2,1)}, f32[2,640,1280]{2,1,0:T(8,128)}, f32[2,640,1280]{2,1,0:T(8,128)}) fusion(bf16[2,640,1280]{2,1,0:T(8,128)(2,1)S(1)} %copy-done.1, f32[]{:T(128)S(6)} %min_shard_map.3, bf16[1,640,1280]{2,1,0:T(8,128)(2,1)} %bitcast.80, bf16[1,640,1280]{2,1,0:T(8,128)(2,1)} %bitcast.78, f32[2,640,1280]{2,1,0:T(8,128)} %param.21, ...), kind=kLoop, calls=%fused_computation.96 | loop fusion | flops 32768000 | bytes 36044804 | tf_op jit(solution)/shard_map/convert_element_type | solution.py:30
  1188.7 1.1 copy-done.6
  1189.9 0.5 copy-done.7
  1190.3 20.4 %fusion.61 = (bf16[2,160,5120]{2,1,0:T(8,128)(2,1)}, f32[2,160,5120]{2,1,0:T(8,128)}, f32[2,160,5120]{2,1,0:T(8,128)}, bf16[2,160,5120]{2,1,0:T(8,128)(2,1)}, f3...) fusion(bf16[2,160,5120]{2,1,0:T(8,128)(2,1)S(1)} %copy-done.2, f32[]{:T(128)S(6)} %min_shard_map.3, ...), kind=kLoop, calls=%fused_computation.87 | loop fusion | flops 65536000 | bytes 72089600 | tf_op jit(solution)/shard_map/convert_element_type | solution.py:30
  (51 shorter events, 0.6 us)
Async XLA Ops:
  7.2 75.4 %all-gather.13.cloned.1.call-start = ((), (), s32[]{:S(2)}) async-start(), calls=%async_computation.12 | async-start | bytes 14745600 | tf_op jit(solution)/shard_map/all_gather | solution.py:40
  11.1 4.1 copy-start
  11.1 142.4 %all-gather.15.cloned.1.call-start = ((), (), s32[]{:S(2)}) async-start(), calls=%async_computation.13 | async-start | bytes 14745600 | tf_op jit(solution)/shard_map/all_gather | solution.py:40
  15.2 209.3 %all-gather.17.cloned.1.call-start = ((), (), s32[]{:S(2)}) async-start(), calls=%async_computation.14 | async-start | bytes 14745600 | tf_op jit(solution)/shard_map/all_gather | solution.py:40
  17.2 278.1 %all-gather.21.cloned.1.call-start = ((), (), s32[]{:S(2)}) async-start(), calls=%async_computation.16 | async-start | bytes 14745600 | tf_op jit(solution)/shard_map/all_gather | solution.py:40
  17.7 348.3 %all-gather.23.cloned.1.call-start = ((), (), s32[]{:S(2)}) async-start(), calls=%async_computation.17 | async-start | bytes 14745600 | tf_op jit(solution)/shard_map/all_gather | solution.py:40
  18.3 418.5 %all-gather.19.cloned.1.call-start = ((), (), s32[]{:S(2)}) async-start(), calls=%async_computation.15 | async-start | bytes 14745600 | tf_op jit(solution)/shard_map/all_gather | solution.py:40
  18.9 836.4 %reduce-scatter.15.cloned.1.call-start = ((), (), s32[]{:S(2)}) async-start(), calls=%async_computation.10 | async-start | bytes 14745600 | tf_op jit(solution)/shard_map/reduce_scatter | solution.py:53
  30.4 123.1 %copy-start.14 = (f32[2048]{0:T(1024)}, f32[2048]{0:T(1024)S(1)}, u32[]{:S(2)}) copy-start(f32[2048]{0:T(1024)S(1)} %add_rsqrt_fusion) | copy-start | bytes 24580
  273.0 56.5 %copy-start.12 = (f32[2048]{0:T(1024)}, f32[2048]{0:T(1024)S(1)}, u32[]{:S(2)}) copy-start(f32[2048]{0:T(1024)S(1)} %get-tuple-element.26) | copy-start | bytes 24580
  273.0 163.9 %copy-start.9 = (f32[2048]{0:T(1024)}, f32[2048]{0:T(1024)S(1)}, u32[]{:S(2)}) copy-start(f32[2048]{0:T(1024)S(1)} %fusion.91) | copy-start | bytes 24580
  496.2 35.7 %copy-start.8 = (bf16[2048,1280]{0,1:T(8,128)(2,1)S(1)}, bf16[2048,1280]{0,1:T(8,128)(2,1)}, u32[]{:S(2)}) copy-start(bf16[2048,1280]{0,1:T(8,128)(2,1)} %get-tuple-element.27) | copy-start | bytes 15728644
  531.9 41.0 %copy-start.13 = (f32[2048]{0:T(1024)S(1)}, f32[2048]{0:T(1024)}, u32[]{:S(2)}) copy-start(f32[2048]{0:T(1024)} %copy-done.12) | copy-start | bytes 24580
  531.9 41.0 %copy-start.10 = (f32[2048]{0:T(1024)S(1)}, f32[2048]{0:T(1024)}, u32[]{:S(2)}) copy-start(f32[2048]{0:T(1024)} %copy-done.9) | copy-start | bytes 24580
  619.1 236.3 %reduce-scatter.17.cloned.1.call-start = ((), (), s32[]{:S(2)}) async-start(), calls=%async_computation.11 | async-start | bytes 14745600 | tf_op jit(solution)/shard_map/reduce_scatter | solution.py:53
  661.0 35.2 %copy-start.15 = (f32[2048]{0:T(1024)S(1)}, f32[2048]{0:T(1024)}, u32[]{:S(2)}) copy-start(f32[2048]{0:T(1024)} %copy-done.14) | copy-start | bytes 24580
  661.1 219.8 %reduce-scatter.11.cloned.1.call-start = ((), (), s32[]{:S(2)}) async-start(), calls=%async_computation.8 | async-start | bytes 14745600 | tf_op jit(solution)/shard_map/reduce_scatter | solution.py:53
  734.3 0.7 copy-start.11
  734.3 234.8 %reduce-scatter.13.cloned.1.call-start = ((), (), s32[]{:S(2)}) async-start(), calls=%async_computation.9 | async-start | bytes 14745600 | tf_op jit(solution)/shard_map/reduce_scatter | solution.py:53
  773.1 284.4 %reduce-scatter.7.cloned.1.call-start = ((), (), s32[]{:S(2)}) async-start(), calls=%async_computation.6 | async-start | bytes 14745600 | tf_op jit(solution)/shard_map/reduce_scatter | solution.py:53
  821.4 324.3 %reduce-scatter.9.cloned.1.call-start = ((), (), s32[]{:S(2)}) async-start(), calls=%async_computation.7 | async-start | bytes 14745600 | tf_op jit(solution)/shard_map/reduce_scatter | solution.py:53
  855.3 319.9 %copy-start.1 = (bf16[2,640,1280]{2,1,0:T(8,128)(2,1)S(1)}, bf16[2,640,1280]{2,1,0:T(8,128)(2,1)}, u32[]{:S(2)}) copy-start(bf16[2,640,1280]{2,1,0:T(8,128)(2,1)} %param.15) | copy-start | bytes 9830404
  1175.2 13.5 %copy-start.2 = (bf16[2,160,5120]{2,1,0:T(8,128)(2,1)S(1)}, bf16[2,160,5120]{2,1,0:T(8,128)(2,1)}, u32[]{:S(2)}) copy-start(bf16[2,160,5120]{2,1,0:T(8,128)(2,1)} %param.13) | copy-start | bytes 9830404
  1175.2 13.5 %copy-start.3 = (bf16[2,160,5120]{2,1,0:T(8,128)(2,1)S(1)}, bf16[2,160,5120]{2,1,0:T(8,128)(2,1)}, u32[]{:S(2)}) copy-start(bf16[2,160,5120]{2,1,0:T(8,128)(2,1)} %param.14) | copy-start | bytes 9830404
  1175.2 13.5 %copy-start.4 = (bf16[160,5120]{1,0:T(8,128)(2,1)S(1)}, bf16[160,5120]{1,0:T(8,128)(2,1)}, u32[]{:S(2)}) copy-start(bf16[160,5120]{1,0:T(8,128)(2,1)} %reduce-scatter.11.cloned.1.call-done) | copy-start | bytes 4915204
  1175.2 13.5 %copy-start.5 = (bf16[160,5120]{1,0:T(8,128)(2,1)S(1)}, bf16[160,5120]{1,0:T(8,128)(2,1)}, u32[]{:S(2)}) copy-start(bf16[160,5120]{1,0:T(8,128)(2,1)} %reduce-scatter.13.cloned.1.call-done) | copy-start | bytes 4915204
  1175.2 14.6 %copy-start.6 = (bf16[160,5120]{1,0:T(8,128)(2,1)S(1)}, bf16[160,5120]{1,0:T(8,128)(2,1)}, u32[]{:S(2)}) copy-start(bf16[160,5120]{1,0:T(8,128)(2,1)} %reduce-scatter.7.cloned.1.call-done) | copy-start | bytes 4915204
  1175.2 15.1 %copy-start.7 = (bf16[160,5120]{1,0:T(8,128)(2,1)S(1)}, bf16[160,5120]{1,0:T(8,128)(2,1)}, u32[]{:S(2)}) copy-start(bf16[160,5120]{1,0:T(8,128)(2,1)} %reduce-scatter.9.cloned.1.call-done) | copy-start | bytes 4915204
Sparse Core Ops, SparseCore 0:
  11.2 71.3 all-gather.12
  85.0 68.4 all-gather.14
  155.9 68.5 all-gather.16
  226.7 68.4 all-gather.20
  297.5 68.4 all-gather.22
  368.3 68.5 all-gather.18
  619.2 84.8 reduce-scatter.14
  707.6 84.8 reduce-scatter.16
  796.0 84.8 reduce-scatter.10
  884.2 84.8 reduce-scatter.12
  972.6 84.8 reduce-scatter.6
  1060.9 84.8 reduce-scatter.8
where the time goes:
time: 1220 us
  matrix products  610 us (50%)
  waiting for transfers between devices  477 us (39%)
  other arithmetic  62.7 us (5%)
  local copies, waits for them, and re-layouts  27.8 us (2%)
  blocking collectives  22.6 us (2%)
  between operations  17.6 us (1%)
    reduce_scatter x6, waiting for transfers between devices, step(): lax.psum_scatter(by_w[name], 'dp', scatter_dimension=0, tiled=True)  282 us
    dot_general x5, matrix products, layer(): gate = jnp.dot(a, w['w_gate'], preferred_element_type=jnp.float32)  212 us
    dot_general x5, matrix products, layer(): up = jnp.dot(a, w['w_up'], preferred_element_type=jnp.float32)  204 us
    all_gather x6, waiting for transfers between devices, fetched(): lax.all_gather(w[number], 'dp', axis=0, tiled=True)  194 us
    dot_general x5, matrix products, matmul(): jnp.dot(a, w, preferred_element_type=jnp.float32).astype(jnp.bfloat16)  194 us
    convert_element_type x2, other arithmetic, adamw(): return ((w - 0.02 * step).astype(jnp.bfloat16), m, v)  33.9 us
  transfers between devices with their start and end apart: 12, of which 10 were waited for; matrix products, arithmetic and copies ran while one was open for 39% of the time, Pallas kernels for 0%

commit v1 on v0

v1 whole, which is shorter than its diff:
```python
import functools

import jax
import jax.numpy as jnp
from jax import lax
from jax.experimental import pallas as pl
from jax.experimental.pallas import tpu as pltpu
from jax.sharding import PartitionSpec as P

F32, BF16 = jnp.float32, jnp.bfloat16
X, Y, C = (1, 0, 0), (0, 1, 0), (0, 0, 1)
DIAGONAL = (1, 1, 0)
MESH = pl.DeviceIdType.MESH
ANY = pl.BlockSpec(memory_space=pl.ANY)
VMEM_LIMIT = 61 * 2**20


def dot(a, b, ca, cb):
    return lax.dot_general(a, b, (((ca,), (cb,)), ((), ())), preferred_element_type=F32)


def place(flip):
    index = lax.axis_index("dp")
    x, y, core = index // 4, index // 2 % 2, index % 2
    return (x + flip[0]) % 2 * 4 + (y + flip[1]) % 2 * 2 + (core + flip[2]) % 2


def remote(src, dst, send, receive, flip):
    return pltpu.make_async_remote_copy(
        src_ref=src, dst_ref=dst, send_sem=send, recv_sem=receive, device_id={"dp": place(flip)}, device_id_type=MESH
    )


def greet():
    barrier = pltpu.get_barrier_semaphore()
    for flip in (X, Y, C):
        pl.semaphore_signal(barrier, inc=1, device_id={"dp": place(flip)}, device_id_type=MESH)
    pl.semaphore_wait(barrier, 3)


class Gather:
    def __init__(self, shard, middle):
        self.inputs, self.middle = [shard], middle
        rows, cols = shard.shape
        self.outputs = [jax.ShapeDtypeStruct((8 * rows, cols), BF16)]
        self.scratch = [pltpu.VMEM((rows, cols), BF16), pltpu.SemaphoreType.DMA((2,)), pltpu.SemaphoreType.DMA((13,)), pltpu.SemaphoreType.DMA((13,))]

    def bind(self, refs_in, refs_out, scratch):
        (self.shard,), (self.full,), (self.held, self.local, self.send, self.receive) = refs_in, refs_out, scratch
        rows = self.shard.shape[0]
        half = rows // 2

        def part(flip, first, count):
            return self.full.at[pl.ds(pl.multiple_of(place(flip) * rows, 16) + first, count)]

        def copy(number, flip, of, first, count):
            src = self.shard.at[pl.ds(first, count)] if of is None else part(of, first, count)
            return remote(src, part(of or (0, 0, 0), first, count), self.send.at[number], self.receive.at[number], flip)

        self.xa, self.xb = copy(0, X, None, 0, half), copy(1, X, None, half, half)
        self.yb, self.ya = copy(2, Y, None, half, half), copy(3, Y, None, 0, half)
        self.low, self.high = copy(4, Y, X, 0, half), copy(5, X, Y, half, half)
        self.own = copy(6, C, None, 0, rows)
        self.cxa, self.cxb = copy(7, C, X, 0, half), copy(8, C, X, half, half)
        self.cyb, self.cya = copy(9, C, Y, half, half), copy(10, C, Y, 0, half)
        self.clow, self.chigh = copy(11, C, DIAGONAL, 0, half), copy(12, C, DIAGONAL, half, half)
        self.load = pltpu.make_async_copy(self.shard, self.held, self.local.at[0])
        self.store = pltpu.make_async_copy(self.held, part((0, 0, 0), 0, rows), self.local.at[1])

    def start(self):
        for one in (self.xa, self.yb, self.xb, self.ya, self.own, self.load):
            one.start()

    def relay(self):
        self.xa.wait_recv()
        self.low.start()
        self.cxa.start()
        self.yb.wait_recv()
        self.high.start()
        self.cyb.start()
        self.load.wait()
        self.store.start()

    def finish(self):
        self.xb.wait_recv()
        self.cxb.start()
        self.ya.wait_recv()
        self.cya.start()
        self.low.wait_recv()
        self.clow.start()
        self.high.wait_recv()
        self.chigh.start()
        for one in (self.own, self.cxa, self.cyb, self.cxb, self.cya, self.clow, self.chigh):
            one.wait_recv()
        for one in (self.xa, self.xb, self.yb, self.ya, self.low, self.high):
            one.wait_send()
        for one in (self.own, self.cxa, self.cyb, self.cxb, self.cya, self.clow, self.chigh):
            one.wait_send()
        self.store.wait()


class Hop:
    def __init__(self, array, left, right):
        self.inputs, self.flips, self.middle = [array], (left, right), None
        self.outputs = [jax.ShapeDtypeStruct(array.shape, array.dtype)]
        self.scratch = [pltpu.SemaphoreType.DMA((2,)), pltpu.SemaphoreType.DMA((2,))]

    def bind(self, refs_in, refs_out, scratch):
        (src,), (dst,), (send, receive) = refs_in, refs_out, scratch
        half = src.shape[1] // 2
        self.copies = [
            remote(src.at[:, pl.ds(i * half, half)], dst.at[:, pl.ds(i * half, half)], send.at[i], receive.at[i], flip)
            for i, flip in enumerate(self.flips)
        ]

    def start(self):
        for one in self.copies:
            one.start()

    def finish(self):
        for one in self.copies:
            one.wait_recv()
        for one in self.copies:
            one.wait_send()


def run(number, steps, compute, ins, outs, comms, scratch=(), flops=0):
    counts = [len(ins)] + [len(c.inputs) for c in comms] + [len(outs)] + [len(c.outputs) for c in comms]
    counts += [len(scratch)] + [len(c.scratch) for c in comms]

    def kernel(*refs):
        refs, groups = list(refs), []
        for count in counts:
            groups.append(refs[:count])
            refs = refs[count:]
        k = len(comms) + 1
        g_in, g_out, g_scratch = groups[:k], groups[k : 2 * k], groups[2 * k :]
        for c, *bound in zip(comms, g_in[1:], g_out[1:], g_scratch[1:]):
            c.bind(*bound)
        step = pl.program_id(0)

        @pl.when(step == 0)
        def _():
            greet()
            for c in comms:
                c.start()

        for c in comms:
            if c.middle is not None:
                pl.when(step == c.middle)(c.relay)
        if compute is not None:
            compute(step, g_in[0], g_out[0], g_scratch[0])

        @pl.when(step == steps - 1)
        def _():
            for c in comms:
                c.finish()

    out = pl.pallas_call(
        kernel,
        grid=(steps,),
        in_specs=[spec for _, spec in ins] + [ANY for c in comms for _ in c.inputs],
        out_specs=[spec for _, spec in outs] + [ANY for c in comms for _ in c.outputs],
        out_shape=[shape for shape, _ in outs] + [shape for c in comms for shape in c.outputs],
        scratch_shapes=list(scratch) + [s for c in comms for s in c.scratch],
        compiler_params=pltpu.CompilerParams(
            collective_id=number, has_side_effects=True, vmem_limit_bytes=VMEM_LIMIT, dimension_semantics=("arbitrary",)
        ),
        cost_estimate=pl.CostEstimate(flops=flops or 10**9, bytes_accessed=5 * 10**7, transcendentals=0),
        name=f"k{number}",
    )(*[a for a, _ in ins], *[a for c in comms for a in c.inputs])
    return out


def shape(rows, cols, dtype=BF16):
    return jax.ShapeDtypeStruct((rows, cols), dtype)


def norm_rows(wide):
    scale = lax.rsqrt(jnp.mean(wide * wide, -1, keepdims=True) + 1e-6)
    return scale, (wide * scale).astype(BF16)


def k_norm(number, h, comms):
    tokens, d = h.shape
    rows = tokens // 4
    block = pl.BlockSpec((rows, d), lambda i: (i, 0))

    def compute(step, ins, outs, _):
        outs[0][...] = norm_rows(ins[0][...].astype(F32))[1]

    return run(number, 4, compute, [(h, block)], [(shape(tokens, d), block)], comms)


def k_gate(number, a, w, comms):
    (tokens, d), ff = a.shape, w.shape[1]
    m, n = tokens // 2, ff // 4

    def compute(step, ins, outs, _):
        outs[0][...] = dot(ins[0][...], ins[1][...], 1, 0)

    return run(
        number, 8, compute,
        [(a, pl.BlockSpec((m, d), lambda i: (i // 4, 0))), (w, pl.BlockSpec((d, n), lambda i: (0, i % 4)))],
        [(shape(tokens, ff, F32), pl.BlockSpec((m, n), lambda i: (i // 4, i % 4)))],
        comms,
    )


def k_up(number, a, w, gate, comms):
    (tokens, d), ff = a.shape, w.shape[1]
    m, n = tokens // 2, ff // 4
    tile = pl.BlockSpec((m, n), lambda i: (i // 4, i % 4))

    def compute(step, ins, outs, _):
        up = dot(ins[0][...], ins[1][...], 1, 0)
        outs[0][...] = up
        outs[1][...] = (jax.nn.silu(ins[2][...]) * up).astype(BF16)

    return run(
        number, 8, compute,
        [(a, pl.BlockSpec((m, d), lambda i: (i // 4, 0))), (w, pl.BlockSpec((d, n), lambda i: (0, i % 4))), (gate, tile)],
        [(shape(tokens, ff, F32), tile), (shape(tokens, ff), tile)],
        comms,
    )


def k_down(number, s, w, h, comms):
    (tokens, ff), d = s.shape, w.shape[1]
    m = tokens // 4
    rows = pl.BlockSpec((m, d), lambda i: (i, 0))

    def compute(step, ins, outs, _):
        new = ins[2][...] + dot(ins[0][...], ins[1][...], 1, 0).astype(BF16)
        outs[0][...] = new
        outs[1][...] = norm_rows(new.astype(F32))[1]

    return run(
        number, 4, compute,
        [(s, pl.BlockSpec((m, ff), lambda i: (i, 0))), (w, pl.BlockSpec((ff, d), lambda i: (0, 0), pipeline_mode=pl.Buffered(1))), (h, rows)],
        [(shape(tokens, d), rows), (shape(tokens, d), rows)],
        comms,
    )


def k_back_gated(number, d_out, w, gate, up, comms):
    (tokens, d), ff = d_out.shape, w.shape[0]
    m, n = tokens // 2, ff // 4
    tile = pl.BlockSpec((m, n), lambda i: (i // 4, i % 4))

    def compute(step, ins, outs, _):
        ds = dot(ins[0][...], ins[1][...], 1, 1).astype(BF16).astype(F32)
        g, u = ins[2][...], ins[3][...]
        sig = jax.nn.sigmoid(g)
        outs[0][...] = (ds * u * (sig * (1 + g * (1 - sig)))).astype(BF16)
        outs[1][...] = (ds * (g * sig)).astype(BF16)

    return run(
        number, 8, compute,
        [(d_out, pl.BlockSpec((m, d), lambda i: (i // 4, 0))), (w, pl.BlockSpec((n, d), lambda i: (i % 4, 0))), (gate, tile), (up, tile)],
        [(shape(tokens, ff), tile), (shape(tokens, ff), tile)],
        comms,
    )


def k_back_in(number, d_gate, w, comms):
    (tokens, ff), d = d_gate.shape, w.shape[0]
    m = tokens // 4
    rows = pl.BlockSpec((m, d), lambda i: (i, 0))

    def compute(step, ins, outs, _):
        outs[0][...] = dot(ins[0][...], ins[1][...], 1, 1).astype(BF16)

    return run(
        number, 4, compute,
        [(d_gate, pl.BlockSpec((m, ff), lambda i: (i, 0))), (w, pl.BlockSpec((d, ff), lambda i: (0, 0), pipeline_mode=pl.Buffered(1)))],
        [(shape(tokens, d), rows)],
        comms,
    )


def k_back_norm(number, d_up, w, other, h, d_out, comms):
    (tokens, ff), d = d_up.shape, w.shape[0]
    m = tokens // 4
    rows = pl.BlockSpec((m, d), lambda i: (i, 0))

    def compute(step, ins, outs, _):
        da = (dot(ins[0][...], ins[1][...], 1, 1).astype(BF16) + ins[2][...]).astype(F32)
        wide = ins[3][...].astype(F32)
        scale, _ = norm_rows(wide)
        inner = jnp.sum(da * wide, -1, keepdims=True) / d
        dh = da * scale - wide * (scale * scale * scale * inner)
        outs[0][...] = ins[4][...] + dh.astype(BF16)

    return run(
        number, 4, compute,
        [(d_up, pl.BlockSpec((m, ff), lambda i: (i, 0))), (w, pl.BlockSpec((d, ff), lambda i: (0, 0), pipeline_mode=pl.Buffered(1))), (other, rows), (h, rows), (d_out, rows)],
        [(shape(tokens, d), rows)],
        comms,
    )


def exchange_scratch(rows, cols):
    return [pltpu.VMEM((4, rows, cols), BF16)] * 2 + [pltpu.SemaphoreType.DMA((4,))] * 2


def exchange(step, theirs, tile, product, scratch, write):
    made, came, send, receive = scratch

    def copy(i):
        return remote(made.at[i], came.at[i], send.at[i], receive.at[i], C)

    for i in range(4):
        pl.when(step == i + 1)(lambda i=i: copy(i).start())

    @pl.when(step < 4)
    def _():
        made[step] = product().astype(BF16)

    for i in range(4):

        @pl.when(step == i + 4)
        def _(i=i):
            total = product()
            copy(i).wait_recv()
            write(i, total + came[i].astype(F32))
            if i == 3:
                for k in range(4):
                    copy(k).wait_send()


def k_gradient_in(number, a_split, d_gate, comms):
    (tokens, d), ff = a_split.shape, d_gate.shape[1]
    rows, n = d // 8, ff // 4
    out = pl.BlockSpec((2 * rows, n), lambda i: (0, jnp.maximum(i - 4, 0)))

    def compute(step, ins, outs, scratch):
        def write(i, total):
            self, y, x, xy = (total[k * rows : (k + 1) * rows] for k in range(4))
            near, far = (x, y) if i < 2 else (y, x)
            outs[0][:rows, :] = near.astype(BF16)
            outs[0][rows:, :] = xy.astype(BF16)
            outs[1][:rows, :] = self
            outs[1][rows:, :] = far

        exchange(step, None, None, lambda: dot(ins[0][...], ins[1][...], 0, 0), scratch, write)

    return run(
        number, 8, compute,
        [(a_split, pl.BlockSpec((tokens, d // 2), lambda i: (0, i // 4))), (d_gate, pl.BlockSpec((tokens, n), lambda i: (0, i % 4)))],
        [(shape(2 * rows, ff), out), (shape(2 * rows, ff, F32), out)],
        comms,
        exchange_scratch(4 * rows, n),
    )


def k_gradient_down(number, s, d_out, comms):
    (tokens, ff), d = s.shape, d_out.shape[1]
    rows, half = ff // 8, d // 2
    whole = pl.BlockSpec((2 * rows, d), lambda i: (0, 0), pipeline_mode=pl.Buffered(1))

    def block(i):
        return 0, place((i // 2 % 2, i % 2, 1 - i // 4))

    def compute(step, ins, outs, scratch):
        send, keep = outs

        def write(i, total):
            if i == 0:
                keep[:rows, :] = total
            elif i == 1:
                keep[rows:, :half] = total[:, :half]
                send[:rows, half:] = total[:, half:].astype(BF16)
            elif i == 2:
                send[:rows, :half] = total[:, :half].astype(BF16)
                keep[rows:, half:] = total[:, half:]
            else:
                send[rows:, :] = total.astype(BF16)

        exchange(step, None, None, lambda: dot(ins[0][...], ins[1][...], 0, 0), scratch, write)

    return run(
        number, 8, compute,
        [(s, pl.BlockSpec((tokens, rows), block)), (d_out, pl.BlockSpec((tokens, d), lambda i: (0, 0), pipeline_mode=pl.Buffered(1)))],
        [(shape(2 * rows, d), whole), (shape(2 * rows, d, F32), whole)],
        comms,
        exchange_scratch(rows, d),
    )


def split_columns(a):
    width = a.shape[1] // 8
    flips = [(i // 2 % 2, i % 2, 1 - i // 4) for i in range(8)]
    return jnp.concatenate([lax.dynamic_slice(a, (0, place(f) * width), (a.shape[0], width)) for f in flips], 1)


def added(keep, got):
    total = keep + got.astype(F32)
    rows = keep.shape[0] // 2
    return total[rows:].astype(BF16), total[:rows]


def last(keep, got):
    g = (keep + got.astype(F32)).astype(BF16)
    wide = g.astype(F32)
    return g, jnp.sum(wide * wide)


def adamw(w, m, v, g):
    m = 0.9 * m + 0.1 * g
    v = 0.95 * v + 0.05 * g * g
    step = m * lax.rsqrt(v + 1e-8) + 0.1 * w
    return (w - 0.02 * step).astype(BF16), m, v


def solution(mesh):
    def step(x, dy, *arrays):
        weights, ms, vs = (arrays[i : i + 3] for i in (0, 3, 6))
        h0, dy = x[0], dy[0]
        (g0, g1), (u0, u1), (d0, d1) = ((w[0], w[1]) for w in weights)

        a0, wg0 = k_norm(0, h0, [Gather(g0, 1)])
        gate0, wu0 = k_gate(1, a0, wg0, [Gather(u0, 4)])
        up0, s0, wd0 = k_up(2, a0, wu0, gate0, [Gather(d0, 4)])
        h1, a1, wg1 = k_down(3, s0, wd0, h0, [Gather(g1, 2)])
        gate1, wu1 = k_gate(4, a1, wg1, [Gather(u1, 4)])
        up1, s1, wd1 = k_up(5, a1, wu1, gate1, [Gather(d1, 4)])
        a0s, a1s = split_columns(a0), split_columns(a1)

        done, total = {}, 0.0

        def finish(name, keep, got):
            nonlocal total
            done[name], square = last(keep, got)
            total += square

        d1_send, d1_keep = k_gradient_down(6, s1, dy, [])
        dgate1, dup1, got = k_back_gated(7, dy, wd1, gate1, up1, [Hop(d1_send, X, Y)])
        d1_send, d1_keep = added(d1_keep, got)
        g1_send, g1_keep, got = k_gradient_in(8, a1s, dgate1, [Hop(d1_send, Y, X)])
        finish("d1", d1_keep, got)
        u1_send, u1_keep, got = k_gradient_in(9, a1s, dup1, [Hop(g1_send, X, Y)])
        g1_send, g1_keep = added(g1_keep, got)
        part, got = k_back_in(10, dgate1, wg1, [Hop(u1_send, X, Y)])
        u1_send, u1_keep = added(u1_keep, got)
        dh1, got_g, got_u = k_back_norm(11, dup1, wu1, part, h1, dy, [Hop(g1_send, Y, X), Hop(u1_send, Y, X)])
        finish("g1", g1_keep, got_g)
        finish("u1", u1_keep, got_u)
        d0_send, d0_keep = k_gradient_down(12, s0, dh1, [])
        dgate0, dup0, got = k_back_gated(13, dh1, wd0, gate0, up0, [Hop(d0_send, X, Y)])
        d0_send, d0_keep = added(d0_keep, got)
        g0_send, g0_keep, got = k_gradient_in(14, a0s, dgate0, [Hop(d0_send, Y, X)])
        finish("d0", d0_keep, got)
        u0_send, u0_keep, got = k_gradient_in(15, a0s, dup0, [Hop(g0_send, X, Y)])
        g0_send, g0_keep = added(g0_keep, got)
        got_g, got = run(16, 1, None, [], [], [Hop(g0_send, Y, X), Hop(u0_send, X, Y)])
        finish("g0", g0_keep, got_g)
        u0_send, u0_keep = added(u0_keep, got)
        (got,) = run(17, 1, None, [], [], [Hop(u0_send, Y, X)])
        finish("u0", u0_keep, got)

        for bit in (1, 2, 4):
            total = total + lax.ppermute(total, "dp", [(i, i ^ bit) for i in range(8)])
        count = 8 * sum(g.size for g in done.values())
        factor = jnp.minimum(1.0, 0.5 * lax.rsqrt(total / count + 1e-30))
        new = []
        for i, name in enumerate("gud"):
            g = jnp.stack([done[name + "0"], done[name + "1"]]).astype(F32) * factor
            new.append(adamw(weights[i].astype(F32), ms[i], vs[i], g))
        return tuple(one[which] for which in range(3) for one in new)

    states, cut = P(("rep", "dp"), None, None), P(None, "dp", None)
    return jax.shard_map(
        step,
        mesh=mesh,
        in_specs=(states, states) + (cut,) * 9,
        out_specs=(P("rep", "dp", None),) * 9,
        check_vma=False,
    )
```

time: 1220 us -> 1120 us (0.918)
  Pallas kernels: 0 us -> 937 us
  matrix products: 610 us -> 0 us
  waiting for transfers between devices: 477 us -> 2.88 us
  local copies, waits for them, and re-layouts: 27.8 us -> 68.9 us
  other arithmetic: 62.7 us -> 90.8 us
  blocking collectives: 22.6 us -> 0 us
    pallas_call x0 -> x18, Pallas kernels: none -> 937 us  [run(): pl.pallas_call(kernel, grid=(steps,), in_specs=[spec for _, spec in ins]...]
    dot_general x15 -> x0, matrix products: 610 us -> none  [the longest x5 212 us: layer(): gate = jnp.dot(a, w['w_gate'], preferred_element_type=jnp.float32)]
    reduce_scatter x6 -> x0, waiting for transfers between devices: 282 us -> none  [step(): lax.psum_scatter(by_w[name], 'dp', scatter_dimension=0, tiled=True)]
    all_gather x6 -> x0, waiting for transfers between devices: 194 us -> none  [fetched(): lax.all_gather(w[number], 'dp', axis=0, tiled=True)]
    another operation x0 -> x6, other arithmetic: none -> 29.4 us  [step(): g = jnp.stack([done[name + '0'], done[name + '1']]).astype(F32) * factor]
    add x0 -> x6, other arithmetic: none -> 26.1 us  [added(): total = keep + got.astype(F32)]
    concatenate x0 -> x2, local copies, waits for them, and re-layouts: none -> 23.2 us  [split_columns(): jnp.concatenate([lax.dynamic_slice(a, (0, place(f) * width), (a.shape[0],...]
    psum x1 -> x0, blocking collectives: 22.6 us -> none  [step(): squares = lax.psum(sum((jnp.sum(g * g) for g in gradients)), 'dp')]
  transfers between devices with their start and end apart: 12 -> 3, of which waited for: 10 -> 3; matrix products, arithmetic and copies ran while one was open for 39% -> 0% of each run, Pallas kernels for 0% -> 0%
where the time goes in v1:
time: 1120 us; the launch traced here: 1110 us
  Pallas kernels  937 us (84%)
  other arithmetic  90.8 us (8%)
  local copies, waits for them, and re-layouts  68.9 us (6%)
    pallas_call x18, Pallas kernels, run(): pl.pallas_call(kernel, grid=(steps,), in_specs=[spec for _, spec in ins]...  937 us
    convert_element_type x3, other arithmetic, adamw(): return ((w - 0.02 * step).astype(BF16), m, v)  35.2 us
    another operation x6, other arithmetic, step(): g = jnp.stack([done[name + '0'], done[name + '1']]).astype(F32) * factor  29.4 us
    add x6, other arithmetic, added(): total = keep + got.astype(F32)  26.1 us
    concatenate x2, local copies, waits for them, and re-layouts, split_columns(): jnp.concatenate([lax.dynamic_slice(a, (0, place(f) * width), (a.shape[0],...  23.2 us
  transfers between devices with their start and end apart: 3, of which 3 were waited for; matrix products, arithmetic and copies ran while one was open for 0% of the time, Pallas kernels for 0%

profile of v1, /device:TPU:0, one launch (start us, length us, event | category | flops | bytes accessed | tf_op | source)
XLA Modules:
  0.0 1112.6 jit_solution(1582625498481768340)
XLA Ops:
  0.8 4.0 slice_bitcast_fusion.2
  4.8 1.9 slice_bitcast_fusion.1
  6.7 1.9 slice_bitcast_fusion
  8.7 63.7 %k0.1 = (bf16[2048,1280]{1,0:T(8,128)(2,1)}, bf16[1280,5120]{1,0:T(8,128)(2,1)}) custom-call(bf16[2048,1280]{1,0:T(8,128)(2,1)} %bitcast.29, bf16[160,5120]{1,0:T(8,128)(2,1)} %get-tuple-element.139.refs_1_), custom_call_target="tpu_custom_call" | custom-call | flops 1000000000 | bytes 50000000 | tf_op jit(solution)/shard_map/k0/pallas_call | solution.py:159
  72.3 64.2 %k1.1 = (f32[2048,5120]{1,0:T(8,128)}, bf16[1280,5120]{1,0:T(8,128)(2,1)}) custom-call(bf16[2048,1280]{1,0:T(8,128)(2,1)} %get-tuple-element.53.refs_0_, bf16[1280,5120]{1,0:T(8,128)(2,1)} %get-tuple-element.54.refs_1_, bf16[160,5120]{1,0:T(8,128)(2,1)} %get-tuple-element.137.refs_2_), custom_call_target="tpu_custom_call" | custom-call | flops 1000000000 | bytes 50000000 | tf_op jit(solution)/shard_map/k1/pallas_call | solution.py:159
  136.5 66.6 %k2.1 = (f32[2048,5120]{1,0:T(8,128)}, bf16[2048,5120]{1,0:T(8,128)(2,1)}, bf16[5120,1280]{1,0:T(8,128)(2,1)}) custom-call(bf16[2048,1280]{1,0:T(8,128)(2,1)} %get-tuple-element.53.refs_0_, bf16[1280,5120]{1,0:T(8,128)(2,1)} %get-tuple-element.55.refs_1_, f32[2048,5120]{1,0:T(8,128)} %get-tuple-element.56.refs_2_, bf16[640,1280]{1,0:T(8,128)(2,1)} %get-tuple-element.135.refs_3_), custom_call_target="tpu_custom_call" | custom-call | flops 1000000000 | bytes 50000000 | tf_op jit(solution)/shard_map/k2/pallas_call | solution.py:159
  203.1 67.2 %k3.1 = (bf16[2048,1280]{1,0:T(8,128)(2,1)}, bf16[2048,1280]{1,0:T(8,128)(2,1)}, bf16[1280,5120]{1,0:T(8,128)(2,1)}) custom-call(bf16[2048,5120]{1,0:T(8,128)(2,1)} %get-tuple-element.57.refs_0_, bf16[5120,1280]{1,0:T(8,128)(2,1)} %get-tuple-element.58.refs_1_, bf16[2048,1280]{1,0:T(8,128)(2,1)} %bitcast.30, bf16[160,5120]{1,0:T(8,128)(2,1)} %get-tuple-element.138.refs_3_), custom_call_target="tpu_custom_call" | custom-call | flops 1000000000 | bytes 50000000 | tf_op jit(solution)/shard_map/k3/pallas_call | solution.py:159
  270.4 78.2 %k4.1 = (f32[2048,5120]{1,0:T(8,128)}, bf16[1280,5120]{1,0:T(8,128)(2,1)}) custom-call(bf16[2048,1280]{1,0:T(8,128)(2,1)} %get-tuple-element.59.refs_0_, bf16[1280,5120]{1,0:T(8,128)(2,1)} %get-tuple-element.60.refs_1_, bf16[160,5120]{1,0:T(8,128)(2,1)} %get-tuple-element.136.refs_2_), custom_call_target="tpu_custom_call" | custom-call | flops 1000000000 | bytes 50000000 | tf_op jit(solution)/shard_map/k4/pallas_call | solution.py:159
  348.6 66.4 %k5.1 = (f32[2048,5120]{1,0:T(8,128)}, bf16[2048,5120]{1,0:T(8,128)(2,1)}, bf16[5120,1280]{1,0:T(8,128)(2,1)}) custom-call(bf16[2048,1280]{1,0:T(8,128)(2,1)} %get-tuple-element.59.refs_0_, bf16[1280,5120]{1,0:T(8,128)(2,1)} %get-tuple-element.61.refs_1_, f32[2048,5120]{1,0:T(8,128)} %get-tuple-element.62.refs_2_, bf16[640,1280]{1,0:T(8,128)(2,1)} %get-tuple-element.134.refs_3_), custom_call_target="tpu_custom_call" | custom-call | flops 1000000000 | bytes 50000000 | tf_op jit(solution)/shard_map/k5/pallas_call | solution.py:159
  415.0 41.3 %k6.1 = (bf16[1280,1280]{1,0:T(8,128)(2,1)}, f32[1280,1280]{1,0:T(8,128)}) custom-call(bf16[2048,5120]{1,0:T(8,128)(2,1)} %get-tuple-element.65.refs_0_, bf16[2048,1280]{1,0:T(8,128)(2,1)} %bitcast.26), custom_call_target="tpu_custom_call" | custom-call | flops 1000000000 | bytes 50000000 | tf_op jit(solution)/shard_map/k6/pallas_call | solution.py:159
  456.3 60.0 %k7.1 = (bf16[2048,5120]{1,0:T(8,128)(2,1)}, bf16[2048,5120]{1,0:T(8,128)(2,1)}, bf16[1280,1280]{1,0:T(8,128)(2,1)}) custom-call(bf16[2048,1280]{1,0:T(8,128)(2,1)} %bitcast.27, bf16[5120,1280]{1,0:T(8,128)(2,1)} %get-tuple-element.63.refs_1_, f32[2048,5120]{1,0:T(8,128)} %get-tuple-element.62.refs_2_, f32[2048,5120]{1,0:T(8,128)} %get-tuple-element.64.refs_3_, ...), custom_call_target="tpu_custom_call" | custom-call | flops 1000000000 | bytes 50000000 | tf_op jit(solution)/shard_map/k7/pallas_call | solution.py:159
  516.2 4.4 convert_add_fusion.5
  520.7 2.8 copy-done
  524.8 16.4 %constant_dynamic-slice_fusion = (bf16[2048,160]{1,0:T(8,128)(2,1)}, bf16[2048,160]{1,0:T(8,128)(2,1)}, bf16[2048,160]{1,0:T(8,128)(2,1)}, bf16[2048,160]{1,0:T(...) fusion(bf16[2048,1280]{1,0:T(8,128)(2,1)} %get-tuple-element.59, ...), kind=kLoop, calls=%fused_computation.66 | loop fusion | bytes 20971552 | tf_op jit(solution)/shard_map/dynamic_slice | solution.py:394
  541.2 11.8 %concatenate.7.refs_0_ = bf16[2048,1280]{1,0:T(8,128)(2,1)} concatenate(bf16[2048,160]{1,0:T(8,128)(2,1)} %get-tuple-element.133, bf16[2048,160]{1,0:T(8,128)(2,1)} %get-tuple-element.132, bf16[2048,160]{1,0:T(8,128)(2,1)} %get-tuple-element.131, bf16[2048,160]{1,0:T(8,128)(2,1)} %get-tuple-element.130, bf16[2048,160]{1,0:T(8,128)(2,1)} %get-tuple-element.129, ...), dimensions={1} | concatenate | bytes 10485760 | tf_op jit(solution)/shard_map/concatenate | solution.py:394
  552.9 38.0 %k8.1 = (bf16[320,5120]{1,0:T(8,128)(2,1)}, f32[320,5120]{1,0:T(8,128)}, bf16[640,1280]{1,0:T(8,128)(2,1)}) custom-call(bf16[2048,1280]{1,0:T(8,128)(2,1)} %concatenate.7.refs_0_, bf16[2048,5120]{1,0:T(8,128)(2,1)} %get-tuple-element.68.refs_1_.refs_0_, bf16[640,1280]{1,0:T(8,128)(2,1)} %slice.149.refs_2_), custom_call_target="tpu_custom_call" | custom-call | flops 1000000000 | bytes 50000000 | tf_op jit(solution)/shard_map/k8/pallas_call | solution.py:159
  591.0 5.0 fusion.20
  595.9 43.0 %k9.1 = (bf16[320,5120]{1,0:T(8,128)(2,1)}, f32[320,5120]{1,0:T(8,128)}, bf16[320,5120]{1,0:T(8,128)(2,1)}) custom-call(bf16[2048,1280]{1,0:T(8,128)(2,1)} %concatenate.7.refs_0_, bf16[2048,5120]{1,0:T(8,128)(2,1)} %get-tuple-element.67.refs_1_.refs_0_, bf16[320,5120]{1,0:T(8,128)(2,1)} %get-tuple-element.71.refs_2_), custom_call_target="tpu_custom_call" | custom-call | flops 1000000000 | bytes 50000000 | tf_op jit(solution)/shard_map/k9/pallas_call | solution.py:159
  638.9 44.9 %k10.1 = (bf16[2048,1280]{1,0:T(8,128)(2,1)}, bf16[320,5120]{1,0:T(8,128)(2,1)}) custom-call(bf16[2048,5120]{1,0:T(8,128)(2,1)} %get-tuple-element.68.refs_1_.refs_0_, bf16[1280,5120]{1,0:T(8,128)(2,1)} %get-tuple-element.60.refs_1_, bf16[320,5120]{1,0:T(8,128)(2,1)} %get-tuple-element.72.refs_2_), custom_call_target="tpu_custom_call" | custom-call | flops 1000000000 | bytes 50000000 | tf_op jit(solution)/shard_map/k10/pallas_call | solution.py:159
  683.8 4.7 convert_add_fusion.3
  688.5 1.6 slice.147.refs_6_
  690.1 4.2 convert_add_fusion.4
  694.4 1.6 slice.148.refs_5_
  696.0 1.7 copy-done.3
  697.7 46.5 %k11.1 = (bf16[2048,1280]{1,0:T(8,128)(2,1)}, bf16[160,5120]{1,0:T(8,128)(2,1)}, bf16[160,5120]{1,0:T(8,128)(2,1)}) custom-call(bf16[2048,5120]{1,0:T(8,128)(2,1)} %get-tuple-element.67.refs_1_.refs_0_, bf16[1280,5120]{1,0:T(8,128)(2,1)} %get-tuple-element.61.refs_1_, bf16[2048,1280]{1,0:T(8,128)(2,1)} %get-tuple-element.73.refs_2_, ...), custom_call_target="tpu_custom_call" | custom-call | flops 1000000000 | bytes 50000000 | tf_op jit(solution)/shard_map/k11/pallas_call | solution.py:159
  744.1 41.6 %k12.1 = (bf16[1280,1280]{1,0:T(8,128)(2,1)}, f32[1280,1280]{1,0:T(8,128)}) custom-call(bf16[2048,5120]{1,0:T(8,128)(2,1)} %get-tuple-element.57.refs_0_, bf16[2048,1280]{1,0:T(8,128)(2,1)} %get-tuple-element.79.refs_1_.refs_0_), custom_call_target="tpu_custom_call" | custom-call | flops 1000000000 | bytes 50000000 | tf_op jit(solution)/shard_map/k12/pallas_call | solution.py:159
  785.8 5.1 fusion.19
  790.9 4.1 fusion.21
  795.0 59.8 %k13.1 = (bf16[2048,5120]{1,0:T(8,128)(2,1)}, bf16[2048,5120]{1,0:T(8,128)(2,1)}, bf16[1280,1280]{1,0:T(8,128)(2,1)}) custom-call(bf16[2048,1280]{1,0:T(8,128)(2,1)} %get-tuple-element.79.refs_1_.refs_0_, bf16[5120,1280]{1,0:T(8,128)(2,1)} %get-tuple-element.58.refs_1_, f32[2048,5120]{1,0:T(8,128)} %get-tuple-element.56.refs_2_, ...), custom_call_target="tpu_custom_call" | custom-call | flops 1000000000 | bytes 50000000 | tf_op jit(solution)/shard_map/k13/pallas_call | solution.py:159
  854.9 4.4 convert_add_fusion.2
  859.3 2.8 copy-done.4
  863.4 11.5 %concatenate.6.refs_0_ = bf16[2048,1280]{1,0:T(8,128)(2,1)} concatenate(bf16[2048,160]{1,0:T(8,128)(2,1)S(1)} %get-tuple-element.140, bf16[2048,160]{1,0:T(8,128)(2,1)S(1)} %get-tuple-element.141, bf16[2048,160]{1,0:T(8,128)(2,1)} %get-tuple-element.142, bf16[2048,160]{1,0:T(8,128)(2,1)} %get-tuple-element.143, bf16[2048,160]{1,0:T(8,128)(2,1)} %get-tuple-element.144, ...), dimensions={1} | concatenate | bytes 10485760 | tf_op jit(solution)/shard_map/concatenate | solution.py:394
  874.9 38.0 %k14.1 = (bf16[320,5120]{1,0:T(8,128)(2,1)}, f32[320,5120]{1,0:T(8,128)}, bf16[640,1280]{1,0:T(8,128)(2,1)}) custom-call(bf16[2048,1280]{1,0:T(8,128)(2,1)} %concatenate.6.refs_0_, bf16[2048,5120]{1,0:T(8,128)(2,1)} %get-tuple-element.82.refs_1_, bf16[640,1280]{1,0:T(8,128)(2,1)} %slice.146.refs_2_), custom_call_target="tpu_custom_call" | custom-call | flops 1000000000 | bytes 50000000 | tf_op jit(solution)/shard_map/k14/pallas_call | solution.py:159
  912.8 5.0 fusion.22
  917.9 43.0 %k15.1 = (bf16[320,5120]{1,0:T(8,128)(2,1)}, f32[320,5120]{1,0:T(8,128)}, bf16[320,5120]{1,0:T(8,128)(2,1)}) custom-call(bf16[2048,1280]{1,0:T(8,128)(2,1)} %concatenate.6.refs_0_, bf16[2048,5120]{1,0:T(8,128)(2,1)} %get-tuple-element.86.refs_1_, bf16[320,5120]{1,0:T(8,128)(2,1)} %get-tuple-element.87.refs_2_), custom_call_target="tpu_custom_call" | custom-call | flops 1000000000 | bytes 50000000 | tf_op jit(solution)/shard_map/k15/pallas_call | solution.py:159
  960.8 4.6 convert_add_fusion.1
  965.4 2.8 copy-done.5
  969.6 55.1 %k16.1 = (bf16[160,5120]{1,0:T(8,128)(2,1)}, bf16[320,5120]{1,0:T(8,128)(2,1)}) custom-call(bf16[160,5120]{1,0:T(8,128)(2,1)} %slice.145.refs_0_, bf16[320,5120]{1,0:T(8,128)(2,1)} %get-tuple-element.89.refs_1_), custom_call_target="tpu_custom_call" | custom-call | flops 1000000000 | bytes 50000000 | tf_op jit(solution)/shard_map/k16/pallas_call | solution.py:159
  1024.7 5.1 fusion.18
  1029.8 3.7 convert_add_fusion
  1033.5 2.8 copy-done.6
  1037.7 20.0 %k17.1 = bf16[160,5120]{1,0:T(8,128)(2,1)} custom-call(bf16[160,5120]{1,0:T(8,128)(2,1)} %slice.144.refs_0_), custom_call_target="tpu_custom_call" | custom-call | flops 1000000000 | bytes 50000000 | tf_op jit(solution)/shard_map/k17/pallas_call | solution.py:159
  1057.7 5.1 fusion.23
  1068.6 2.3 collective-permute-start.1
  1072.8 2.3 collective-permute-start.2
  1077.1 13.5 %fusion.8 = (bf16[2,640,1280]{2,1,0:T(8,128)(2,1)}, f32[2,640,1280]{2,1,0:T(8,128)}, f32[2,640,1280]{2,1,0:T(8,128)}) fusion(bf16[2,640,1280]{2,1,0:T(8,128)(2,1)S(1)} %copy-done.8, f32[]{:T(128)S(6)} %min_shard_map.3, bf16[1,640,1280]{2,1,0:T(8,128)(2,1)} %get-tuple-element.108, bf16[1,640,1280]{2,1,0:T(8,128)(2,1)} %get-tuple-element.106, ...), kind=kLoop, calls=%fused_computation.17 | loop fusion | flops 32768000 | bytes 36044804 | tf_op jit(solution)/shard_map/convert_element_type | solution.py:413
  1090.6 12.7 %fusion.5 = (bf16[2,160,5120]{2,1,0:T(8,128)(2,1)}, f32[2,160,5120]{2,1,0:T(8,128)}, f32[2,160,5120]{2,1,0:T(8,128)}) fusion(bf16[2,160,5120]{2,1,0:T(8,128)(2,1)S(1)} %copy-done.10, f32[]{:T(128)S(6)} %min_shard_map.3, bf16[1,160,5120]{2,1,0:T(8,128)(2,1)} %get-tuple-element.112, bf16[1,160,5120]{2,1,0:T(8,128)(2,1)} %get-tuple-element.110, ...), kind=kLoop, calls=%fused_computation.14 | loop fusion | flops 32768000 | bytes 36044804 | tf_op jit(solution)/shard_map/convert_element_type | solution.py:413
  1103.3 9.1 fusion.2
  (44 shorter events, 9.2 us)
Async XLA Ops:
  0.6 4.2 copy-start.9
  0.8 5.9 copy-start.7
  520.7 2.8 copy-start
  683.8 6.3 slice-start.4
  683.8 6.3 slice-start.5
  688.5 5.8 copy-start.1
  694.4 3.3 copy-start.3
  785.8 5.2 copy-start.2
  859.3 2.8 copy-start.4
  965.4 2.8 copy-start.5
  1024.7 5.1 copy-start.12
  1033.5 2.8 copy-start.6
  1057.7 19.3 %copy-start.8 = (bf16[2,640,1280]{2,1,0:T(8,128)(2,1)S(1)}, bf16[2,640,1280]{2,1,0:T(8,128)(2,1)}, u32[]{:S(2)}) copy-start(bf16[2,640,1280]{2,1,0:T(8,128)(2,1)} %param.15) | copy-start | bytes 9830404
  1066.8 1.1 collective-permute-start
  1068.6 3.6 collective-permute-start.1
  1072.8 3.6 collective-permute-start.2
  1077.1 13.5 %copy-start.10 = (bf16[2,160,5120]{2,1,0:T(8,128)(2,1)S(1)}, bf16[2,160,5120]{2,1,0:T(8,128)(2,1)}, u32[]{:S(2)}) copy-start(bf16[2,160,5120]{2,1,0:T(8,128)(2,1)} %param.14) | copy-start | bytes 9830404
  1077.1 26.2 %slice-start = ((s8[6553600]{0:T(1024)(128)(4,1)}), s8[4194304]{0:T(1024)(128)(4,1)S(1)}, s32[]{:S(2)}) async-start(s8[6553600]{0:T(1024)(128)(4,1)} %bitcast.31), calls=%async_computation | async-start | bytes 8388608
  1077.1 26.2 %slice-start.2 = ((s8[6553600]{0:T(1024)(128)(4,1)}), s8[4194304]{0:T(1024)(128)(4,1)S(1)}, s32[]{:S(2)}) async-start(s8[6553600]{0:T(1024)(128)(4,1)} %bitcast.33), calls=%async_computation.2 | async-start | bytes 8388608
  1090.6 12.7 %copy-start.11 = (bf16[2,160,5120]{2,1,0:T(8,128)(2,1)S(1)}, bf16[2,160,5120]{2,1,0:T(8,128)(2,1)}, u32[]{:S(2)}) copy-start(bf16[2,160,5120]{2,1,0:T(8,128)(2,1)} %param.13) | copy-start | bytes 9830404
  1090.6 12.8 %slice-start.1 = ((s8[6553600]{0:T(1024)(128)(4,1)}), s8[2359296]{0:T(1024)(128)(4,1)S(1)}, s32[]{:S(2)}) async-start(s8[6553600]{0:T(1024)(128)(4,1)} %bitcast.31), calls=%async_computation.1 | async-start | bytes 4718592
  1090.6 12.7 %slice-start.3 = ((s8[6553600]{0:T(1024)(128)(4,1)}), s8[2359296]{0:T(1024)(128)(4,1)S(1)}, s32[]{:S(2)}) async-start(s8[6553600]{0:T(1024)(128)(4,1)} %bitcast.33), calls=%async_computation.3 | async-start | bytes 4718592

commit v2 on v1

--- a/solution.py
+++ b/solution.py
@@ -1,5 +1,3 @@
-import functools
-
 import jax
 import jax.numpy as jnp
 from jax import lax
@@ -12,7 +10,7 @@
 DIAGONAL = (1, 1, 0)
 MESH = pl.DeviceIdType.MESH
 ANY = pl.BlockSpec(memory_space=pl.ANY)
-VMEM_LIMIT = 61 * 2**20
+VMEM_LIMIT = 63 * 2**20
 
 
 def dot(a, b, ca, cb):
@@ -124,8 +122,50 @@
             one.wait_send()
 
 
-def run(number, steps, compute, ins, outs, comms, scratch=(), flops=0):
-    counts = [len(ins)] + [len(c.inputs) for c in comms] + [len(outs)] + [len(c.outputs) for c in comms]
+class AddHop:
+    def __init__(self, keep, got, left, right, middle):
+        self.inputs, self.flips, self.middle = [keep, got], (left, right), middle
+        rows, cols = keep.shape[0] // 2, keep.shape[1]
+        self.outputs = [jax.ShapeDtypeStruct((rows, cols), F32), jax.ShapeDtypeStruct((rows, cols), BF16)]
+        self.scratch = [pltpu.VMEM(keep.shape, F32), pltpu.VMEM(got.shape, BF16), pltpu.VMEM((rows, cols), BF16), pltpu.SemaphoreType.DMA((3,))]
+        self.scratch += [pltpu.SemaphoreType.DMA((2,)), pltpu.SemaphoreType.DMA((2,))]
+
+    def bind(self, refs_in, refs_out, scratch):
+        (keep, got), (stay, dst), (self.sum, self.came, self.out, local, send, receive) = refs_in, refs_out, scratch
+        self.rows, half = dst.shape[0], dst.shape[1] // 2
+        self.loads = [pltpu.make_async_copy(keep, self.sum, local.at[0]), pltpu.make_async_copy(got, self.came, local.at[1])]
+        self.store = pltpu.make_async_copy(self.sum.at[pl.ds(0, self.rows)], stay, local.at[2])
+        self.copies = [
+            remote(self.out.at[:, pl.ds(i * half, half)], dst.at[:, pl.ds(i * half, half)], send.at[i], receive.at[i], flip)
+            for i, flip in enumerate(self.flips)
+        ]
+
+    def start(self):
+        for one in self.loads:
+            one.start()
+
+    def relay(self):
+        for one in self.loads:
+            one.wait()
+        rows = self.rows
+        self.out[...] = (self.sum[rows:, :] + self.came[rows:, :].astype(F32)).astype(BF16)
+        self.sum[:rows, :] = self.sum[:rows, :] + self.came[:rows, :].astype(F32)
+        self.store.start()
+        for one in self.copies:
+            one.start()
+
+    def finish(self):
+        for one in self.copies:
+            one.wait_recv()
+        for one in self.copies:
+            one.wait_send()
+        self.store.wait()
+
+
+def run(number, steps, compute, ins, outs, comms, scratch=(), flops=0, sides=()):
+    sides = [side(steps) for side in sides]
+    counts = [len(ins)] + [len(s[0]) for s in sides] + [len(c.inputs) for c in comms]
+    counts += [len(outs)] + [len(s[1]) for s in sides] + [len(c.outputs) for c in comms]
     counts += [len(scratch)] + [len(c.scratch) for c in comms]
 
     def kernel(*refs):
@@ -133,9 +173,9 @@
         for count in counts:
             groups.append(refs[:count])
             refs = refs[count:]
-        k = len(comms) + 1
+        n, k = len(sides), len(sides) + len(comms) + 1
         g_in, g_out, g_scratch = groups[:k], groups[k : 2 * k], groups[2 * k :]
-        for c, *bound in zip(comms, g_in[1:], g_out[1:], g_scratch[1:]):
+        for c, *bound in zip(comms, g_in[1 + n :], g_out[1 + n :], g_scratch[1:]):
             c.bind(*bound)
         step = pl.program_id(0)
 
@@ -150,13 +190,17 @@
                 pl.when(step == c.middle)(c.relay)
         if compute is not None:
             compute(step, g_in[0], g_out[0], g_scratch[0])
+        for s, s_in, s_out in zip(sides, g_in[1:], g_out[1:]):
+            s[2](s_in, s_out)
 
         @pl.when(step == steps - 1)
         def _():
             for c in comms:
                 c.finish()
 
-    out = pl.pallas_call(
+    ins = list(ins) + [one for s in sides for one in s[0]]
+    outs = list(outs) + [one for s in sides for one in s[1]]
+    return pl.pallas_call(
         kernel,
         grid=(steps,),
         in_specs=[spec for _, spec in ins] + [ANY for c in comms for _ in c.inputs],
@@ -169,7 +213,31 @@
         cost_estimate=pl.CostEstimate(flops=flops or 10**9, bytes_accessed=5 * 10**7, transcendentals=0),
         name=f"k{number}",
     )(*[a for a, _ in ins], *[a for c in comms for a in c.inputs])
-    return out
+
+
+def blocks(rows, cols, steps):
+    n = min(steps, 8)
+    per = steps // n
+    if rows % (16 * n) == 0:
+        return tuple(pl.BlockSpec((rows // n, cols), lambda i, k=k: (i // per + k * n, 0)) for k in (0, 1)) + (n, pl.BlockSpec((8, cols), lambda i: (i // per, 0)))
+    return tuple(pl.BlockSpec((rows, cols // n), lambda i, k=k: (k, i // per)) for k in (0, 1)) + (1, pl.BlockSpec((8, cols // n), lambda i: (0, i // per)))
+
+
+def side_last(keep, got):
+    rows, cols = keep.shape
+
+    def side(steps):
+        low, _, n, sums = blocks(rows, cols, steps)
+
+        def compute(ins, outs):
+            g = (ins[0][...] + ins[1][...].astype(F32)).astype(BF16)
+            outs[0][...] = g
+            wide = g.astype(F32)
+            outs[1][...] = jnp.sum((wide * wide).reshape(-1, 8, wide.shape[1]), 0)
+
+        return [(keep, low), (got, low)], [(shape(rows, cols), low), (shape(8 * n, cols, F32), sums)], compute
+
+    return side
 
 
 def shape(rows, cols, dtype=BF16):
@@ -179,6 +247,16 @@
 def norm_rows(wide):
     scale = lax.rsqrt(jnp.mean(wide * wide, -1, keepdims=True) + 1e-6)
     return scale, (wide * scale).astype(BF16)
+
+
+def choose(step, chosen):
+    width = chosen.shape[1] // 8
+
+    @pl.when(step == 0)
+    def _():
+        away = lax.broadcasted_iota(jnp.int32, (chosen.shape[0], width), 0) - lax.broadcasted_iota(jnp.int32, (chosen.shape[0], width), 1)
+        for i in range(8):
+            chosen[:, i * width : (i + 1) * width] = jnp.where(away == place((i // 2 % 2, i % 2, 1 - i // 4)) * width, 1.0, 0.0).astype(BF16)
 
 
 def k_norm(number, h, comms):
@@ -186,10 +264,13 @@
     rows = tokens // 4
     block = pl.BlockSpec((rows, d), lambda i: (i, 0))
 
-    def compute(step, ins, outs, _):
-        outs[0][...] = norm_rows(ins[0][...].astype(F32))[1]
-
-    return run(number, 4, compute, [(h, block)], [(shape(tokens, d), block)], comms)
+    def compute(step, ins, outs, scratch):
+        choose(step, scratch[0])
+        a = norm_rows(ins[0][...].astype(F32))[1]
+        outs[0][...] = a
+        outs[1][...] = dot(a, scratch[0][...], 1, 0).astype(BF16)
+
+    return run(number, 4, compute, [(h, block)], [(shape(tokens, d), block)] * 2, comms, [pltpu.VMEM((d, d), BF16)])
 
 
 def k_gate(number, a, w, comms):
@@ -230,106 +311,53 @@
     m = tokens // 4
     rows = pl.BlockSpec((m, d), lambda i: (i, 0))
 
-    def compute(step, ins, outs, _):
+    def compute(step, ins, outs, scratch):
+        choose(step, scratch[0])
         new = ins[2][...] + dot(ins[0][...], ins[1][...], 1, 0).astype(BF16)
+        a = norm_rows(new.astype(F32))[1]
         outs[0][...] = new
-        outs[1][...] = norm_rows(new.astype(F32))[1]
+        outs[1][...] = a
+        outs[2][...] = dot(a, scratch[0][...], 1, 0).astype(BF16)
 
     return run(
         number, 4, compute,
         [(s, pl.BlockSpec((m, ff), lambda i: (i, 0))), (w, pl.BlockSpec((ff, d), lambda i: (0, 0), pipeline_mode=pl.Buffered(1))), (h, rows)],
-        [(shape(tokens, d), rows), (shape(tokens, d), rows)],
+        [(shape(tokens, d), rows)] * 3,
         comms,
-    )
-
-
-def k_back_gated(number, d_out, w, gate, up, comms):
-    (tokens, d), ff = d_out.shape, w.shape[0]
-    m, n = tokens // 2, ff // 4
-    tile = pl.BlockSpec((m, n), lambda i: (i // 4, i % 4))
-
-    def compute(step, ins, outs, _):
-        ds = dot(ins[0][...], ins[1][...], 1, 1).astype(BF16).astype(F32)
-        g, u = ins[2][...], ins[3][...]
-        sig = jax.nn.sigmoid(g)
-        outs[0][...] = (ds * u * (sig * (1 + g * (1 - sig)))).astype(BF16)
-        outs[1][...] = (ds * (g * sig)).astype(BF16)
-
-    return run(
-        number, 8, compute,
-        [(d_out, pl.BlockSpec((m, d), lambda i: (i // 4, 0))), (w, pl.BlockSpec((n, d), lambda i: (i % 4, 0))), (gate, tile), (up, tile)],
-        [(shape(tokens, ff), tile), (shape(tokens, ff), tile)],
-        comms,
-    )
-
-
-def k_back_in(number, d_gate, w, comms):
-    (tokens, ff), d = d_gate.shape, w.shape[0]
-    m = tokens // 4
-    rows = pl.BlockSpec((m, d), lambda i: (i, 0))
-
-    def compute(step, ins, outs, _):
-        outs[0][...] = dot(ins[0][...], ins[1][...], 1, 1).astype(BF16)
-
-    return run(
-        number, 4, compute,
-        [(d_gate, pl.BlockSpec((m, ff), lambda i: (i, 0))), (w, pl.BlockSpec((d, ff), lambda i: (0, 0), pipeline_mode=pl.Buffered(1)))],
-        [(shape(tokens, d), rows)],
-        comms,
-    )
-
-
-def k_back_norm(number, d_up, w, other, h, d_out, comms):
-    (tokens, ff), d = d_up.shape, w.shape[0]
-    m = tokens // 4
-    rows = pl.BlockSpec((m, d), lambda i: (i, 0))
-
-    def compute(step, ins, outs, _):
-        da = (dot(ins[0][...], ins[1][...], 1, 1).astype(BF16) + ins[2][...]).astype(F32)
-        wide = ins[3][...].astype(F32)
-        scale, _ = norm_rows(wide)
-        inner = jnp.sum(da * wide, -1, keepdims=True) / d
-        dh = da * scale - wide * (scale * scale * scale * inner)
-        outs[0][...] = ins[4][...] + dh.astype(BF16)
-
-    return run(
-        number, 4, compute,
-        [(d_up, pl.BlockSpec((m, ff), lambda i: (i, 0))), (w, pl.BlockSpec((d, ff), lambda i: (0, 0), pipeline_mode=pl.Buffered(1))), (other, rows), (h, rows), (d_out, rows)],
-        [(shape(tokens, d), rows)],
-        comms,
-    )
-
-
-def exchange_scratch(rows, cols):
-    return [pltpu.VMEM((4, rows, cols), BF16)] * 2 + [pltpu.SemaphoreType.DMA((4,))] * 2
-
-
-def exchange(step, theirs, tile, product, scratch, write):
+        [pltpu.VMEM((d, d), BF16)],
+    )
+
+
+def exchange_scratch(n, rows, cols):
+    return [pltpu.VMEM((n, rows, cols), BF16)] * 2 + [pltpu.SemaphoreType.DMA((n,))] * 2
+
+
+def exchange(step, n, product, scratch, write):
     made, came, send, receive = scratch
 
     def copy(i):
         return remote(made.at[i], came.at[i], send.at[i], receive.at[i], C)
 
-    for i in range(4):
+    for i in range(n):
         pl.when(step == i + 1)(lambda i=i: copy(i).start())
-
-    @pl.when(step < 4)
+    total = product()
+
+    @pl.when(step < n)
     def _():
-        made[step] = product().astype(BF16)
-
-    for i in range(4):
-
-        @pl.when(step == i + 4)
+        made[step] = total.astype(BF16)
+
+    for i in range(n):
+
+        @pl.when(step == i + n)
         def _(i=i):
-            total = product()
             copy(i).wait_recv()
             write(i, total + came[i].astype(F32))
-            if i == 3:
-                for k in range(4):
+            if i == n - 1:
+                for k in range(n):
                     copy(k).wait_send()
 
 
-def k_gradient_in(number, a_split, d_gate, comms):
+def k_gradient_in(number, a_split, d_gate, comms, sides=()):
     (tokens, d), ff = a_split.shape, d_gate.shape[1]
     rows, n = d // 8, ff // 4
     out = pl.BlockSpec((2 * rows, n), lambda i: (0, jnp.maximum(i - 4, 0)))
@@ -343,18 +371,19 @@
             outs[1][:rows, :] = self
             outs[1][rows:, :] = far
 
-        exchange(step, None, None, lambda: dot(ins[0][...], ins[1][...], 0, 0), scratch, write)
+        exchange(step, 4, lambda: dot(ins[0][...], ins[1][...], 0, 0), scratch, write)
 
     return run(
         number, 8, compute,
         [(a_split, pl.BlockSpec((tokens, d // 2), lambda i: (0, i // 4))), (d_gate, pl.BlockSpec((tokens, n), lambda i: (0, i % 4)))],
         [(shape(2 * rows, ff), out), (shape(2 * rows, ff, F32), out)],
         comms,
-        exchange_scratch(4 * rows, n),
-    )
-
-
-def k_gradient_down(number, s, d_out, comms):
+        exchange_scratch(4, 4 * rows, n),
+        sides=sides,
+    )
+
+
+def k_gradient_down(number, s, d_out, comms, sides=()):
     (tokens, ff), d = s.shape, d_out.shape[1]
     rows, half = ff // 8, d // 2
     whole = pl.BlockSpec((2 * rows, d), lambda i: (0, 0), pipeline_mode=pl.Buffered(1))
@@ -377,33 +406,154 @@
             else:
                 send[rows:, :] = total.astype(BF16)
 
-        exchange(step, None, None, lambda: dot(ins[0][...], ins[1][...], 0, 0), scratch, write)
+        exchange(step, 4, lambda: dot(ins[0][...], ins[1][...], 0, 0), scratch, write)
 
     return run(
         number, 8, compute,
         [(s, pl.BlockSpec((tokens, rows), block)), (d_out, pl.BlockSpec((tokens, d), lambda i: (0, 0), pipeline_mode=pl.Buffered(1)))],
         [(shape(2 * rows, d), whole), (shape(2 * rows, d, F32), whole)],
         comms,
-        exchange_scratch(rows, d),
-    )
-
-
-def split_columns(a):
-    width = a.shape[1] // 8
-    flips = [(i // 2 % 2, i % 2, 1 - i // 4) for i in range(8)]
-    return jnp.concatenate([lax.dynamic_slice(a, (0, place(f) * width), (a.shape[0], width)) for f in flips], 1)
-
-
-def added(keep, got):
-    total = keep + got.astype(F32)
-    rows = keep.shape[0] // 2
-    return total[rows:].astype(BF16), total[:rows]
-
-
-def last(keep, got):
-    g = (keep + got.astype(F32)).astype(BF16)
-    wide = g.astype(F32)
-    return g, jnp.sum(wide * wide)
+        exchange_scratch(4, rows, d),
+        sides=sides,
+    )
+
+
+def k_back_gated(number, d_out, w, gate, up, comms, sides=()):
+    (tokens, d), ff = d_out.shape, w.shape[0]
+    m, n = tokens // 2, ff // 4
+    tile = pl.BlockSpec((m, n), lambda i: (i // 4, i % 4))
+
+    def compute(step, ins, outs, _):
+        ds = dot(ins[0][...], ins[1][...], 1, 1).astype(BF16).astype(F32)
+        g, u = ins[2][...], ins[3][...]
+        sig = jax.nn.sigmoid(g)
+        acted = g * sig
+        outs[0][...] = (ds * u * (sig * (1 + (g - acted)))).astype(BF16)
+        outs[1][...] = (ds * acted).astype(BF16)
+
+    return run(
+        number, 8, compute,
+        [(d_out, pl.BlockSpec((m, d), lambda i: (i // 4, 0))), (w, pl.BlockSpec((n, d), lambda i: (i % 4, 0))), (gate, tile), (up, tile)],
+        [(shape(tokens, ff), tile), (shape(tokens, ff), tile)],
+        comms,
+        sides=sides,
+    )
+
+
+def k_back_norm(number, d_gate, w_gate, d_up, w_up, h, d_out, comms, sides=()):
+    (tokens, ff), d = d_up.shape, w_up.shape[0]
+    m = tokens // 8
+    rows = pl.BlockSpec((m, d), lambda i: (i, 0))
+    wide_rows = pl.BlockSpec((m, ff), lambda i: (i, 0))
+    matrix = pl.BlockSpec((d, ff), lambda i: (0, 0), pipeline_mode=pl.Buffered(1))
+
+    def compute(step, ins, outs, _):
+        da = dot(ins[0][...], ins[1][...], 1, 1).astype(BF16)
+        da = (da + dot(ins[2][...], ins[3][...], 1, 1).astype(BF16)).astype(F32)
+        wide = ins[4][...].astype(F32)
+        scale, _ = norm_rows(wide)
+        inner = jnp.sum(da * wide, -1, keepdims=True) / d
+        dh = da * scale - wide * (scale * scale * scale * inner)
+        outs[0][...] = ins[5][...] + dh.astype(BF16)
+
+    return run(
+        number, 8, compute,
+        [(d_gate, wide_rows), (w_gate, matrix), (d_up, wide_rows), (w_up, matrix), (h, rows), (d_out, rows)],
+        [(shape(tokens, d), rows)],
+        comms,
+        sides=sides,
+    )
+
+
+def k_tail(number, u_send, u_keep, d_got, d_keep, g_got, g_keep, squares):
+    (rows2, cols), (d_rows, d_cols) = u_keep.shape, d_keep.shape
+    rows, half, quarter = rows2 // 2, cols // 2, cols // 4
+    others = [(i // 4, i // 2 % 2, i % 2) for i in range(1, 8)]
+
+    def kernel(*refs):
+        u_s, u_k, d_g, d_k, g_g, g_k, sq_in, u_out, d_out, g_out, sq_out = refs[:11]
+        uk, uc, u2, uc2, dk, dc, gk, gg, g2, gc, slots, mine, local, send, receive = refs[11:]
+        barrier = pltpu.get_barrier_semaphore()
+        for flip in others:
+            pl.semaphore_signal(barrier, inc=1, device_id={"dp": place(flip)}, device_id_type=MESH)
+        pl.semaphore_wait(barrier, len(others))
+
+        def copy(i, src, dst, flip):
+            return remote(src, dst, send.at[i], receive.at[i], flip)
+
+        def part(ref, i, n):
+            size = ref.shape[1] // n
+            return ref.at[:, pl.ds(i * size, size)]
+
+        first = [copy(i, part(u_s, i, 4), part(uc, i, 4), X if i < 2 else Y) for i in range(4)]
+        g_hop = [copy(4 + i, part(g2, i, 2), part(gc, i, 2), (Y, X)[i]) for i in range(2)]
+        second = [copy(6 + i, part(u2, i, 4), part(uc2, i, 4), Y if i < 2 else X) for i in range(4)]
+        for i in (0, 2, 1, 3):
+            first[i].start()
+        loads = [pltpu.make_async_copy(s, t, local.at[i]) for i, (s, t) in enumerate(((g_k, gk), (g_g, gg), (u_k, uk), (d_k, dk), (d_g, dc)))]
+        for one in loads:
+            one.start()
+        loads[0].wait()
+        loads[1].wait()
+        g2[...] = (gk[rows:, :] + gg[rows:, :].astype(F32)).astype(BF16)
+        gk[:rows, :] = gk[:rows, :] + gg[:rows, :].astype(F32)
+        for one in g_hop:
+            one.start()
+        loads[2].wait()
+        for i in (0, 2, 1, 3):
+            at = pl.ds(i * quarter, quarter)
+            first[i].wait_recv()
+            u2[:, at] = (uk[rows:, at] + uc[rows:, at].astype(F32)).astype(BF16)
+            uk[:rows, at] = uk[:rows, at] + uc[:rows, at].astype(F32)
+            second[i].start()
+
+        total = sq_in[...]
+
+        def final(out, keep, came, at):
+            g = (keep[: came.shape[0], at] + came[:, at].astype(F32)).astype(BF16)
+            out[:, at] = g
+            wide = g.astype(F32)
+            wide = jnp.sum((wide * wide).reshape(-1, 8, wide.shape[1]), 0)
+            return sum(wide[:, k : k + 128] for k in range(0, wide.shape[1], 128))
+
+        loads[3].wait()
+        loads[4].wait()
+        total += final(d_out, dk, dc, pl.ds(0, d_cols))
+        for i in range(2):
+            g_hop[i].wait_recv()
+            total += final(g_out, gk, gc, pl.ds(i * half, half))
+        for i in (0, 2, 1, 3):
+            second[i].wait_recv()
+            total += final(u_out, uk, uc2, pl.ds(i * quarter, quarter))
+        mine[...] = total
+        me = place((0, 0, 0))
+        spread = [copy(10 + i, mine, slots.at[me], flip) for i, flip in enumerate(others)]
+        for one in spread:
+            one.start()
+        slots[me] = total
+        for one in spread:
+            one.wait_recv()
+        sq_out[...] = sum(slots[i] for i in range(8))
+        for one in first + g_hop + second + spread:
+            one.wait_send()
+
+    vmem = pl.BlockSpec(memory_space=pltpu.VMEM)
+    return pl.pallas_call(
+        kernel,
+        in_specs=[ANY] * 6 + [vmem],
+        out_specs=[vmem] * 4,
+        out_shape=[shape(rows, cols), shape(d_rows, d_cols), shape(rows, cols), shape(8, 128, F32)],
+        scratch_shapes=[
+            pltpu.VMEM((rows2, cols), F32), pltpu.VMEM((rows2, cols), BF16), pltpu.VMEM((rows, cols), BF16), pltpu.VMEM((rows, cols), BF16),
+            pltpu.VMEM((d_rows, d_cols), F32), pltpu.VMEM((d_rows, d_cols), BF16),
+            pltpu.VMEM((rows2, cols), F32), pltpu.VMEM((rows2, cols), BF16), pltpu.VMEM((rows, cols), BF16), pltpu.VMEM((rows, cols), BF16),
+            pltpu.VMEM((8, 8, 128), F32), pltpu.VMEM((8, 128), F32),
+            pltpu.SemaphoreType.DMA((5,)), pltpu.SemaphoreType.DMA((17,)), pltpu.SemaphoreType.DMA((17,)),
+        ],
+        compiler_params=pltpu.CompilerParams(collective_id=number, has_side_effects=True, vmem_limit_bytes=VMEM_LIMIT),
+        cost_estimate=pl.CostEstimate(flops=10**9, bytes_accessed=5 * 10**7, transcendentals=0),
+        name=f"k{number}",
+    )(u_send, u_keep, d_got, d_keep, g_got, g_keep, squares)
 
 
 def adamw(w, m, v, g):
@@ -419,48 +569,33 @@
         h0, dy = x[0], dy[0]
         (g0, g1), (u0, u1), (d0, d1) = ((w[0], w[1]) for w in weights)
 
-        a0, wg0 = k_norm(0, h0, [Gather(g0, 1)])
+        a0, a0s, wg0 = k_norm(0, h0, [Gather(g0, 1)])
         gate0, wu0 = k_gate(1, a0, wg0, [Gather(u0, 4)])
         up0, s0, wd0 = k_up(2, a0, wu0, gate0, [Gather(d0, 4)])
-        h1, a1, wg1 = k_down(3, s0, wd0, h0, [Gather(g1, 2)])
+        h1, a1, a1s, wg1 = k_down(3, s0, wd0, h0, [Gather(g1, 2)])
         gate1, wu1 = k_gate(4, a1, wg1, [Gather(u1, 4)])
         up1, s1, wd1 = k_up(5, a1, wu1, gate1, [Gather(d1, 4)])
-        a0s, a1s = split_columns(a0), split_columns(a1)
 
         done, total = {}, 0.0
-
-        def finish(name, keep, got):
-            nonlocal total
-            done[name], square = last(keep, got)
-            total += square
-
         d1_send, d1_keep = k_gradient_down(6, s1, dy, [])
         dgate1, dup1, got = k_back_gated(7, dy, wd1, gate1, up1, [Hop(d1_send, X, Y)])
-        d1_send, d1_keep = added(d1_keep, got)
-        g1_send, g1_keep, got = k_gradient_in(8, a1s, dgate1, [Hop(d1_send, Y, X)])
-        finish("d1", d1_keep, got)
+        g1_send, g1_keep, d1_keep, got_d = k_gradient_in(8, a1s, dgate1, [AddHop(d1_keep, got, Y, X, 1)])
         u1_send, u1_keep, got = k_gradient_in(9, a1s, dup1, [Hop(g1_send, X, Y)])
-        g1_send, g1_keep = added(g1_keep, got)
-        part, got = k_back_in(10, dgate1, wg1, [Hop(u1_send, X, Y)])
-        u1_send, u1_keep = added(u1_keep, got)
-        dh1, got_g, got_u = k_back_norm(11, dup1, wu1, part, h1, dy, [Hop(g1_send, Y, X), Hop(u1_send, Y, X)])
-        finish("g1", g1_keep, got_g)
-        finish("u1", u1_keep, got_u)
-        d0_send, d0_keep = k_gradient_down(12, s0, dh1, [])
-        dgate0, dup0, got = k_back_gated(13, dh1, wd0, gate0, up0, [Hop(d0_send, X, Y)])
-        d0_send, d0_keep = added(d0_keep, got)
-        g0_send, g0_keep, got = k_gradient_in(14, a0s, dgate0, [Hop(d0_send, Y, X)])
-        finish("d0", d0_keep, got)
-        u0_send, u0_keep, got = k_gradient_in(15, a0s, dup0, [Hop(g0_send, X, Y)])
-        g0_send, g0_keep = added(g0_keep, got)
-        got_g, got = run(16, 1, None, [], [], [Hop(g0_send, Y, X), Hop(u0_send, X, Y)])
-        finish("g0", g0_keep, got_g)
-        u0_send, u0_keep = added(u0_keep, got)
-        (got,) = run(17, 1, None, [], [], [Hop(u0_send, Y, X)])
-        finish("u0", u0_keep, got)
-
-        for bit in (1, 2, 4):
-            total = total + lax.ppermute(total, "dp", [(i, i ^ bit) for i in range(8)])
+        dh1, done["d1"], sums, g1_keep, got_g, got = k_back_norm(
+            10, dgate1, wg1, dup1, wu1, h1, dy, [AddHop(g1_keep, got, Y, X, 1), Hop(u1_send, X, Y)], [side_last(d1_keep, got_d)]
+        )
+        total += jnp.sum(sums)
+        d0_send, d0_keep, done["g1"], sums, u1_keep, got_u = k_gradient_down(
+            11, s0, dh1, [AddHop(u1_keep, got, Y, X, 1)], [side_last(g1_keep, got_g)]
+        )
+        total += jnp.sum(sums)
+        dgate0, dup0, done["u1"], sums, got = k_back_gated(12, dh1, wd0, gate0, up0, [Hop(d0_send, X, Y)], [side_last(u1_keep, got_u)])
+        total += jnp.sum(sums)
+        g0_send, g0_keep, d0_keep, got_d = k_gradient_in(13, a0s, dgate0, [AddHop(d0_keep, got, Y, X, 1)])
+        u0_send, u0_keep, got = k_gradient_in(14, a0s, dup0, [Hop(g0_send, X, Y)])
+        squares = jnp.zeros((8, 128), F32).at[0, 0].set(total)
+        done["u0"], done["d0"], done["g0"], squares = k_tail(15, u0_send, u0_keep, got_d, d0_keep, got, g0_keep, squares)
+        total = jnp.sum(squares)
         count = 8 * sum(g.size for g in done.values())
         factor = jnp.minimum(1.0, 0.5 * lax.rsqrt(total / count + 1e-30))
         new = []

time: 1120 us -> 974 us (0.87)
  local copies, waits for them, and re-layouts: 68.9 us -> 10.5 us
  other arithmetic: 90.8 us -> 40.4 us
  Pallas kernels: 937 us -> 912 us
    pallas_call x18 -> x15, Pallas kernels: 937 us -> 832 us  [run(): pl.pallas_call(kernel, grid=(steps,), in_specs=[spec for _, spec in ins]...]
    pallas_call x0 -> x1, Pallas kernels: none -> 80.4 us  [k_tail(): pl.pallas_call(kernel, in_specs=[ANY] * 6 + [vmem], out_specs=[vmem] * 4,...]
    another operation x6 -> x0, other arithmetic: 29.4 us -> none  [step(): g = jnp.stack([done[name + '0'], done[name + '1']]).astype(F32) * factor]
    add x6 -> x0, other arithmetic: 26.1 us -> none  [added(): total = keep + got.astype(F32)]
    concatenate x2 -> x0, local copies, waits for them, and re-layouts: 23.2 us -> none  [split_columns(): jnp.concatenate([lax.dynamic_slice(a, (0, place(f) * width), (a.shape[0],...]
    dynamic_slice x1 -> x0, local copies, waits for them, and re-layouts: 16.4 us -> none  [split_columns(): lax.dynamic_slice(a, (0, place(f) * width), (a.shape[0], width))]
    convert_element_type x3 -> x2, other arithmetic: 35.2 us -> 34.3 us  [adamw(): return ((w - 0.02 * step).astype(BF16), m, v)]
  transfers between devices with their start and end apart: 3 -> 0, of which waited for: 3 -> 0; matrix products, arithmetic and copies ran while one was open for 0% -> 0% of each run, Pallas kernels for 0% -> 0%
where the time goes in v2:
time: 974 us; the launch traced here: 967 us
  Pallas kernels  912 us (94%)
  other arithmetic  40.4 us (4%)
  local copies, waits for them, and re-layouts  10.5 us (1%)
    pallas_call x15, Pallas kernels, run(): pl.pallas_call(kernel, grid=(steps,), in_specs=[spec for _, spec in ins]...  832 us
    pallas_call x1, Pallas kernels, k_tail(): pl.pallas_call(kernel, in_specs=[ANY] * 6 + [vmem], out_specs=[vmem] * 4,...  80.4 us
    convert_element_type x2, other arithmetic, adamw(): return ((w - 0.02 * step).astype(BF16), m, v)  34.3 us

profile of v2, /device:TPU:0, one launch (start us, length us, event | category | flops | bytes accessed | tf_op | source)
XLA Modules:
  0.0 967.2 jit_solution(17937733461492889275)
XLA Ops:
  0.6 0.0 copy-start.2
  0.7 0.0 copy-start
  0.7 4.0 slice_bitcast_fusion.2
  4.7 0.0 copy-done.2
  4.7 1.9 slice_bitcast_fusion.1
  6.6 0.0 copy-done
  6.6 1.9 slice_bitcast_fusion
  8.5 64.2 %k0.1 = (bf16[2048,1280]{1,0:T(8,128)(2,1)}, bf16[2048,1280]{1,0:T(8,128)(2,1)}, bf16[1280,5120]{1,0:T(8,128)(2,1)}) custom-call(bf16[2048,1280]{1,0:T(8,128)(2,1)} %bitcast.24, bf16[160,5120]{1,0:T(8,128)(2,1)} %get-tuple-element.149.refs_1_), custom_call_target="tpu_custom_call" | custom-call | flops 1000000000 | bytes 50000000 | tf_op jit(solution)/shard_map/k0/pallas_call | solution.py:203
  72.7 64.1 %k1.1 = (f32[2048,5120]{1,0:T(8,128)}, bf16[1280,5120]{1,0:T(8,128)(2,1)}) custom-call(bf16[2048,1280]{1,0:T(8,128)(2,1)} %get-tuple-element.79.refs_0_, bf16[1280,5120]{1,0:T(8,128)(2,1)} %get-tuple-element.80.refs_1_, bf16[160,5120]{1,0:T(8,128)(2,1)} %get-tuple-element.147.refs_2_), custom_call_target="tpu_custom_call" | custom-call | flops 1000000000 | bytes 50000000 | tf_op jit(solution)/shard_map/k1/pallas_call | solution.py:203
  136.8 66.5 %k2.1 = (f32[2048,5120]{1,0:T(8,128)}, bf16[2048,5120]{1,0:T(8,128)(2,1)}, bf16[5120,1280]{1,0:T(8,128)(2,1)}) custom-call(bf16[2048,1280]{1,0:T(8,128)(2,1)} %get-tuple-element.79.refs_0_, bf16[1280,5120]{1,0:T(8,128)(2,1)} %get-tuple-element.81.refs_1_, f32[2048,5120]{1,0:T(8,128)} %get-tuple-element.82.refs_2_, bf16[640,1280]{1,0:T(8,128)(2,1)} %get-tuple-element.145.refs_3_), custom_call_target="tpu_custom_call" | custom-call | flops 1000000000 | bytes 50000000 | tf_op jit(solution)/shard_map/k2/pallas_call | solution.py:203
  203.3 67.8 %k3.1 = (bf16[2048,1280]{1,0:T(8,128)(2,1)}, bf16[2048,1280]{1,0:T(8,128)(2,1)}, bf16[2048,1280]{1,0:T(8,128)(2,1)}, bf16[1280,5120]{1,0:T(8,128)(2,1)}) custom-call(bf16[2048,5120]{1,0:T(8,128)(2,1)} %get-tuple-element.83.refs_0_, bf16[5120,1280]{1,0:T(8,128)(2,1)} %get-tuple-element.84.refs_1_, bf16[2048,1280]{1,0:T(8,128)(2,1)} %bitcast.25, ...), custom_call_target="tpu_custom_call" | custom-call | flops 1000000000 | bytes 50000000 | tf_op jit(solution)/shard_map/k3/pallas_call | solution.py:203
  271.1 64.2 %k4.1 = (f32[2048,5120]{1,0:T(8,128)}, bf16[1280,5120]{1,0:T(8,128)(2,1)}) custom-call(bf16[2048,1280]{1,0:T(8,128)(2,1)} %get-tuple-element.85.refs_0_, bf16[1280,5120]{1,0:T(8,128)(2,1)} %get-tuple-element.86.refs_1_, bf16[160,5120]{1,0:T(8,128)(2,1)} %get-tuple-element.146.refs_2_), custom_call_target="tpu_custom_call" | custom-call | flops 1000000000 | bytes 50000000 | tf_op jit(solution)/shard_map/k4/pallas_call | solution.py:203
  335.3 66.7 %k5.1 = (f32[2048,5120]{1,0:T(8,128)}, bf16[2048,5120]{1,0:T(8,128)(2,1)}, bf16[5120,1280]{1,0:T(8,128)(2,1)}) custom-call(bf16[2048,1280]{1,0:T(8,128)(2,1)} %get-tuple-element.85.refs_0_, bf16[1280,5120]{1,0:T(8,128)(2,1)} %get-tuple-element.87.refs_1_.refs_3_, f32[2048,5120]{1,0:T(8,128)} %get-tuple-element.88.refs_2_, ...), custom_call_target="tpu_custom_call" | custom-call | flops 1000000000 | bytes 50000000 | tf_op jit(solution)/shard_map/k5/pallas_call | solution.py:203
  402.0 40.4 %k6.1 = (bf16[1280,1280]{1,0:T(8,128)(2,1)}, f32[1280,1280]{1,0:T(8,128)}) custom-call(bf16[2048,5120]{1,0:T(8,128)(2,1)} %get-tuple-element.91.refs_0_, bf16[2048,1280]{1,0:T(8,128)(2,1)} %bitcast.21), custom_call_target="tpu_custom_call" | custom-call | flops 1000000000 | bytes 50000000 | tf_op jit(solution)/shard_map/k6/pallas_call | solution.py:203
  442.4 59.1 %k7.1 = (bf16[2048,5120]{1,0:T(8,128)(2,1)}, bf16[2048,5120]{1,0:T(8,128)(2,1)}, bf16[1280,1280]{1,0:T(8,128)(2,1)}) custom-call(bf16[2048,1280]{1,0:T(8,128)(2,1)} %bitcast.22, bf16[5120,1280]{1,0:T(8,128)(2,1)} %get-tuple-element.89.refs_1_, f32[2048,5120]{1,0:T(8,128)} %get-tuple-element.88.refs_2_, f32[2048,5120]{1,0:T(8,128)} %get-tuple-element.90.refs_3_, ...), custom_call_target="tpu_custom_call" | custom-call | flops 1000000000 | bytes 50000000 | tf_op jit(solution)/shard_map/k7/pallas_call | solution.py:203
  501.5 38.3 %k8.1 = (bf16[320,5120]{1,0:T(8,128)(2,1)}, f32[320,5120]{1,0:T(8,128)}, f32[640,1280]{1,0:T(8,128)}, bf16[640,1280]{1,0:T(8,128)(2,1)}) custom-call(bf16[2048,1280]{1,0:T(8,128)(2,1)} %get-tuple-element.96.refs_0_, bf16[2048,5120]{1,0:T(8,128)(2,1)} %get-tuple-element.93.refs_1_.refs_0_, f32[1280,1280]{1,0:T(8,128)} %get-tuple-element.97.refs_2_, ...), custom_call_target="tpu_custom_call" | custom-call | flops 1000000000 | bytes 50000000 | tf_op jit(solution)/shard_map/k8/pallas_call | solution.py:203
  539.9 42.4 %k9.1 = (bf16[320,5120]{1,0:T(8,128)(2,1)}, f32[320,5120]{1,0:T(8,128)}, bf16[320,5120]{1,0:T(8,128)(2,1)}) custom-call(bf16[2048,1280]{1,0:T(8,128)(2,1)} %get-tuple-element.96.refs_0_, bf16[2048,5120]{1,0:T(8,128)(2,1)} %get-tuple-element.94.refs_1_.refs_2_, bf16[320,5120]{1,0:T(8,128)(2,1)} %get-tuple-element.102.refs_2_), custom_call_target="tpu_custom_call" | custom-call | flops 1000000000 | bytes 50000000 | tf_op jit(solution)/shard_map/k9/pallas_call | solution.py:203
  582.3 74.7 %k10.1 = (bf16[2048,1280]{1,0:T(8,128)(2,1)}, bf16[640,1280]{1,0:T(8,128)(2,1)}, f32[64,1280]{1,0:T(8,128)}, f32[160,5120]{1,0:T(8,128)}, bf16[160,5120]{1,0:T(8,128)(2,1)}, /*index=5*/bf16[320,5120]{1,0:T(8,128)(2,1)}) custom-call(bf16[2048,5120]{1,0:T(8,128)(2,1)} %get-tuple-element.93.refs_1_.refs_0_, bf16[1280,5120]{1,0:T(8,128)(2,1)} %get-tuple-element.86.refs_1_, ...), custom_call_target="tpu_custom_call" | custom-call | flops 1000000000 | bytes 50000000 | tf_op jit(solution)/shard_map/k10/pallas_call | solution.py:203
  657.0 1.7 reduce_sum.36
  658.7 42.1 %k11.1 = (bf16[1280,1280]{1,0:T(8,128)(2,1)}, f32[1280,1280]{1,0:T(8,128)}, bf16[160,5120]{1,0:T(8,128)(2,1)}, f32[8,5120]{1,0:T(8,128)}, f32[160,5120]{1,0:T(8,128)}, /*index=5*/bf16[160,5120]{1,0:T(8,128)(2,1)}) custom-call(bf16[2048,5120]{1,0:T(8,128)(2,1)} %get-tuple-element.83.refs_0_, bf16[2048,1280]{1,0:T(8,128)(2,1)} %get-tuple-element.105.refs_1_.refs_0_, ...), custom_call_target="tpu_custom_call" | custom-call | flops 1000000000 | bytes 50000000 | tf_op jit(solution)/shard_map/k11/pallas_call | solution.py:203
  700.7 1.6 reduce_sum.37
  703.6 60.8 %k12.1 = (bf16[2048,5120]{1,0:T(8,128)(2,1)}, bf16[2048,5120]{1,0:T(8,128)(2,1)}, bf16[160,5120]{1,0:T(8,128)(2,1)}, f32[8,5120]{1,0:T(8,128)}, bf16[1280,1280]{1,0:T(8,128)(2,1)}) custom-call(bf16[2048,1280]{1,0:T(8,128)(2,1)} %get-tuple-element.105.refs_1_.refs_0_, bf16[5120,1280]{1,0:T(8,128)(2,1)} %get-tuple-element.84.refs_1_, ...), custom_call_target="tpu_custom_call" | custom-call | flops 1000000000 | bytes 50000000 | tf_op jit(solution)/shard_map/k12/pallas_call | solution.py:203
  764.4 1.6 reduce_sum.38
  766.6 0.6 scatter.4.refs_6_
  767.2 38.0 %k13.1 = (bf16[320,5120]{1,0:T(8,128)(2,1)}, f32[320,5120]{1,0:T(8,128)}, f32[640,1280]{1,0:T(8,128)}, bf16[640,1280]{1,0:T(8,128)(2,1)}) custom-call(bf16[2048,1280]{1,0:T(8,128)(2,1)} %get-tuple-element.78.refs_0_, bf16[2048,5120]{1,0:T(8,128)(2,1)} %get-tuple-element.115.refs_1_, f32[1280,1280]{1,0:T(8,128)} %get-tuple-element.116.refs_2_, ...), custom_call_target="tpu_custom_call" | custom-call | flops 1000000000 | bytes 50000000 | tf_op jit(solution)/shard_map/k13/pallas_call | solution.py:203
  805.2 42.6 %k14.1 = (bf16[320,5120]{1,0:T(8,128)(2,1)}, f32[320,5120]{1,0:T(8,128)}, bf16[320,5120]{1,0:T(8,128)(2,1)}) custom-call(bf16[2048,1280]{1,0:T(8,128)(2,1)} %get-tuple-element.78.refs_0_, bf16[2048,5120]{1,0:T(8,128)(2,1)} %get-tuple-element.114.refs_1_, bf16[320,5120]{1,0:T(8,128)(2,1)} %get-tuple-element.118.refs_2_), custom_call_target="tpu_custom_call" | custom-call | flops 1000000000 | bytes 50000000 | tf_op jit(solution)/shard_map/k14/pallas_call | solution.py:203
  847.8 80.4 %k15.1 = (bf16[160,5120]{1,0:T(8,128)(2,1)}, bf16[640,1280]{1,0:T(8,128)(2,1)}, bf16[160,5120]{1,0:T(8,128)(2,1)}, f32[8,128]{1,0:T(8,128)}) custom-call(bf16[320,5120]{1,0:T(8,128)(2,1)} %get-tuple-element.119.refs_0_, f32[320,5120]{1,0:T(8,128)} %get-tuple-element.120.refs_1_, bf16[640,1280]{1,0:T(8,128)(2,1)} %get-tuple-element.121.refs_2_, ...), custom_call_target="tpu_custom_call" | custom-call | flops 1000000000 | bytes 50000000 | tf_op jit(solution)/shard_map/k15/pallas_call | solution.py:541
  928.3 1.3 reduce_sum.39
  930.3 0.0 copy-start.1
  930.3 0.0 copy-start.3
  930.3 0.0 copy-start.4
  930.3 0.0 copy-start.5
  930.3 0.0 copy-start.6
  930.3 0.0 copy-start.7
  930.3 13.9 %fusion.8 = (bf16[2,640,1280]{2,1,0:T(8,128)(2,1)}, f32[2,640,1280]{2,1,0:T(8,128)}, f32[2,640,1280]{2,1,0:T(8,128)}) fusion(bf16[2,640,1280]{2,1,0:T(8,128)(2,1)} %param.17, f32[]{:T(128)S(6)} %min_shard_map.3, bf16[1,640,1280]{2,1,0:T(8,128)(2,1)} %bitcast.26, bf16[1,640,1280]{2,1,0:T(8,128)(2,1)} %bitcast.31, f32[2,640,1280]{2,1,0:T(8,128)} %param.23, ...), kind=kLoop, calls=%fused_computation.17 | loop fusion | flops 32768000 | bytes 36044804 | tf_op jit(solution)/shard_map/convert_element_type | solution.py:563
  944.2 0.0 copy-done.1
  944.2 0.0 copy-done.3
  944.2 0.0 copy-done.4
  944.3 1.1 copy-done.5
  945.4 0.5 copy-done.6
  945.9 0.5 copy-done.7
  946.3 20.4 %fusion.2 = (bf16[2,160,5120]{2,1,0:T(8,128)(2,1)}, f32[2,160,5120]{2,1,0:T(8,128)}, f32[2,160,5120]{2,1,0:T(8,128)}, bf16[2,160,5120]{2,1,0:T(8,128)(2,1)}, f32...) fusion(bf16[2,160,5120]{2,1,0:T(8,128)(2,1)S(1)} %copy-done.1, f32[]{:T(128)S(6)} %min_shard_map.3, ...), kind=kLoop, calls=%fused_computation.11 | loop fusion | flops 65536000 | bytes 72089600 | tf_op jit(solution)/shard_map/convert_element_type | solution.py:563
Async XLA Ops:
  0.6 4.0 copy-start.2
  0.7 5.9 copy-start
  930.3 14.0 %copy-start.1 = (bf16[2,160,5120]{2,1,0:T(8,128)(2,1)S(1)}, bf16[2,160,5120]{2,1,0:T(8,128)(2,1)}, u32[]{:S(2)}) copy-start(bf16[2,160,5120]{2,1,0:T(8,128)(2,1)} %param.15) | copy-start | bytes 9830404
  930.3 14.0 %copy-start.3 = (bf16[2,160,5120]{2,1,0:T(8,128)(2,1)S(1)}, bf16[2,160,5120]{2,1,0:T(8,128)(2,1)}, u32[]{:S(2)}) copy-start(bf16[2,160,5120]{2,1,0:T(8,128)(2,1)} %param.16) | copy-start | bytes 9830404
  930.3 14.0 %copy-start.4 = (bf16[160,5120]{1,0:T(8,128)(2,1)S(1)}, bf16[160,5120]{1,0:T(8,128)(2,1)}, u32[]{:S(2)}) copy-start(bf16[160,5120]{1,0:T(8,128)(2,1)} %get-tuple-element.129) | copy-start | bytes 4915204
  930.3 15.1 %copy-start.5 = (bf16[160,5120]{1,0:T(8,128)(2,1)S(1)}, bf16[160,5120]{1,0:T(8,128)(2,1)}, u32[]{:S(2)}) copy-start(bf16[160,5120]{1,0:T(8,128)(2,1)} %get-tuple-element.132) | copy-start | bytes 4915204
  930.3 15.5 %copy-start.6 = (bf16[160,5120]{1,0:T(8,128)(2,1)S(1)}, bf16[160,5120]{1,0:T(8,128)(2,1)}, u32[]{:S(2)}) copy-start(bf16[160,5120]{1,0:T(8,128)(2,1)} %get-tuple-element.131) | copy-start | bytes 4915204
  930.3 16.0 %copy-start.7 = (bf16[160,5120]{1,0:T(8,128)(2,1)S(1)}, bf16[160,5120]{1,0:T(8,128)(2,1)}, u32[]{:S(2)}) copy-start(bf16[160,5120]{1,0:T(8,128)(2,1)} %get-tuple-element.128) | copy-start | bytes 4915204

commit v3 on v2

--- a/solution.py
+++ b/solution.py
@@ -9,6 +9,8 @@
 X, Y, C = (1, 0, 0), (0, 1, 0), (0, 0, 1)
 DIAGONAL = (1, 1, 0)
 MESH = pl.DeviceIdType.MESH
+ALL = ...
+COST = pl.CostEstimate(flops=10**9, bytes_accessed=5 * 10**7, transcendentals=0)
 ANY = pl.BlockSpec(memory_space=pl.ANY)
 VMEM_LIMIT = 63 * 2**20
 
@@ -37,33 +39,36 @@
 
 
 class Gather:
-    def __init__(self, shard, middle):
-        self.inputs, self.middle = [shard], middle
-        rows, cols = shard.shape
-        self.outputs = [jax.ShapeDtypeStruct((8 * rows, cols), BF16)]
-        self.scratch = [pltpu.VMEM((rows, cols), BF16), pltpu.SemaphoreType.DMA((2,)), pltpu.SemaphoreType.DMA((13,)), pltpu.SemaphoreType.DMA((13,))]
+    def __init__(self, w, layer, middle, rest=True):
+        self.inputs, self.middle, self.layer, self.rest = [w.reshape(-1, w.shape[2])], middle, layer, rest
+        _, self.rows, cols = w.shape
+        self.outputs = [jax.ShapeDtypeStruct((8 * self.rows, cols), BF16)]
+        self.scratch = [pltpu.VMEM((self.rows, cols), BF16), pltpu.SemaphoreType.DMA((2,)), pltpu.SemaphoreType.DMA((17,)), pltpu.SemaphoreType.DMA((17,))]
 
     def bind(self, refs_in, refs_out, scratch):
-        (self.shard,), (self.full,), (self.held, self.local, self.send, self.receive) = refs_in, refs_out, scratch
-        rows = self.shard.shape[0]
-        half = rows // 2
-
-        def part(flip, first, count):
-            return self.full.at[pl.ds(pl.multiple_of(place(flip) * rows, 16) + first, count)]
-
-        def copy(number, flip, of, first, count):
-            src = self.shard.at[pl.ds(first, count)] if of is None else part(of, first, count)
-            return remote(src, part(of or (0, 0, 0), first, count), self.send.at[number], self.receive.at[number], flip)
-
-        self.xa, self.xb = copy(0, X, None, 0, half), copy(1, X, None, half, half)
-        self.yb, self.ya = copy(2, Y, None, half, half), copy(3, Y, None, 0, half)
-        self.low, self.high = copy(4, Y, X, 0, half), copy(5, X, Y, half, half)
-        self.own = copy(6, C, None, 0, rows)
-        self.cxa, self.cxb = copy(7, C, X, 0, half), copy(8, C, X, half, half)
-        self.cyb, self.cya = copy(9, C, Y, half, half), copy(10, C, Y, 0, half)
-        self.clow, self.chigh = copy(11, C, DIAGONAL, 0, half), copy(12, C, DIAGONAL, half, half)
-        self.load = pltpu.make_async_copy(self.shard, self.held, self.local.at[0])
-        self.store = pltpu.make_async_copy(self.held, part((0, 0, 0), 0, rows), self.local.at[1])
+        (w,), (self.full,), (held, local, self.send, self.receive) = refs_in, refs_out, scratch
+        half, rows = self.rows // 2, self.rows
+        self.shard = w.at[pl.ds(self.layer * rows, rows)]
+        self.xa, self.xb = self.copy(0, X, None, 0, half), self.copy(1, X, None, half, half)
+        self.yb, self.ya = self.copy(2, Y, None, half, half), self.copy(3, Y, None, 0, half)
+        self.own = self.copy(4, C, None, 0, rows)
+        self.cxa, self.cxb = self.copy(5, C, X, 0, half), self.copy(6, C, X, half, half)
+        self.cyb, self.cya = self.copy(7, C, Y, half, half), self.copy(8, C, Y, 0, half)
+        self.bind_rest(9)
+        self.load = pltpu.make_async_copy(self.shard, held, local.at[0])
+        self.store = pltpu.make_async_copy(held, self.part((0, 0, 0), 0, rows), local.at[1])
+
+    def part(self, flip, first, count):
+        return self.full.at[pl.ds(pl.multiple_of(place(flip) * self.rows, 8) + first, count)]
+
+    def copy(self, number, flip, of, first, count):
+        src = self.shard.at[pl.ds(first, count)] if of is None else self.part(of, first, count)
+        return remote(src, self.part(of or (0, 0, 0), first, count), self.send.at[number], self.receive.at[number], flip)
+
+    def bind_rest(self, number):
+        q = self.rows // 4
+        self.far = [self.copy(number + i, (Y, X)[i % 2], (X, Y)[i % 2], (i % 2 * 2 + i // 2) * q, q) for i in range(4)]
+        self.across = [self.copy(number + 4 + i, C, DIAGONAL, (i % 2 * 2 + i // 2) * q, q) for i in range(4)]
 
     def start(self):
         for one in (self.xa, self.yb, self.xb, self.ya, self.own, self.load):
@@ -71,30 +76,64 @@
 
     def relay(self):
         self.xa.wait_recv()
-        self.low.start()
+        if self.rest:
+            self.far[0].start()
+            self.far[2].start()
         self.cxa.start()
         self.yb.wait_recv()
-        self.high.start()
+        if self.rest:
+            self.far[1].start()
+            self.far[3].start()
         self.cyb.start()
         self.load.wait()
         self.store.start()
+
+    def finish_rest(self):
+        for far, across in zip(self.far, self.across):
+            far.wait_recv()
+            across.start()
+
+    def wait_rest(self):
+        for one in self.across:
+            one.wait_recv()
+        for one in self.far + self.across:
+            one.wait_send()
 
     def finish(self):
         self.xb.wait_recv()
         self.cxb.start()
         self.ya.wait_recv()
         self.cya.start()
-        self.low.wait_recv()
-        self.clow.start()
-        self.high.wait_recv()
-        self.chigh.start()
-        for one in (self.own, self.cxa, self.cyb, self.cxb, self.cya, self.clow, self.chigh):
+        if self.rest:
+            self.finish_rest()
+        for one in (self.own, self.cxa, self.cyb, self.cxb, self.cya):
             one.wait_recv()
-        for one in (self.xa, self.xb, self.yb, self.ya, self.low, self.high):
+        for one in (self.xa, self.xb, self.yb, self.ya, self.own, self.cxa, self.cyb, self.cxb, self.cya):
             one.wait_send()
-        for one in (self.own, self.cxa, self.cyb, self.cxb, self.cya, self.clow, self.chigh):
-            one.wait_send()
+        if self.rest:
+            self.wait_rest()
         self.store.wait()
+
+
+class GatherRest(Gather):
+    def __init__(self, full, middle):
+        self.inputs, self.middle, self.rows = [full], middle, full.shape[0] // 8
+        self.outputs = [jax.ShapeDtypeStruct(full.shape, BF16)]
+        self.scratch = [pltpu.SemaphoreType.DMA((8,)), pltpu.SemaphoreType.DMA((8,))]
+
+    def bind(self, refs_in, refs_out, scratch):
+        (self.full,), (self.send, self.receive) = refs_out, scratch
+        self.bind_rest(0)
+
+    def start(self):
+        for one in self.far:
+            one.start()
+
+    def relay(self):
+        self.finish_rest()
+
+    def finish(self):
+        self.wait_rest()
 
 
 class Hop:
@@ -148,7 +187,7 @@
         for one in self.loads:
             one.wait()
         rows = self.rows
-        self.out[...] = (self.sum[rows:, :] + self.came[rows:, :].astype(F32)).astype(BF16)
+        self.out[ALL] = (self.sum[rows:, :] + self.came[rows:, :].astype(F32)).astype(BF16)
         self.sum[:rows, :] = self.sum[:rows, :] + self.came[:rows, :].astype(F32)
         self.store.start()
         for one in self.copies:
@@ -162,7 +201,7 @@
         self.store.wait()
 
 
-def run(number, steps, compute, ins, outs, comms, scratch=(), flops=0, sides=()):
+def run(number, steps, compute, ins, outs, comms, scratch=(), sides=()):
     sides = [side(steps) for side in sides]
     counts = [len(ins)] + [len(s[0]) for s in sides] + [len(c.inputs) for c in comms]
     counts += [len(outs)] + [len(s[1]) for s in sides] + [len(c.outputs) for c in comms]
@@ -200,9 +239,15 @@
 
     ins = list(ins) + [one for s in sides for one in s[0]]
     outs = list(outs) + [one for s in sides for one in s[1]]
+    at_in, at_out, aliases = len(ins), len(outs), {}
+    for c in comms:
+        if isinstance(c, GatherRest):
+            aliases[at_in] = at_out
+        at_in, at_out = at_in + len(c.inputs), at_out + len(c.outputs)
     return pl.pallas_call(
         kernel,
         grid=(steps,),
+        input_output_aliases=aliases,
         in_specs=[spec for _, spec in ins] + [ANY for c in comms for _ in c.inputs],
         out_specs=[spec for _, spec in outs] + [ANY for c in comms for _ in c.outputs],
         out_shape=[shape for shape, _ in outs] + [shape for c in comms for shape in c.outputs],
@@ -210,7 +255,7 @@
         compiler_params=pltpu.CompilerParams(
             collective_id=number, has_side_effects=True, vmem_limit_bytes=VMEM_LIMIT, dimension_semantics=("arbitrary",)
         ),
-        cost_estimate=pl.CostEstimate(flops=flops or 10**9, bytes_accessed=5 * 10**7, transcendentals=0),
+        cost_estimate=COST,
         name=f"k{number}",
     )(*[a for a, _ in ins], *[a for c in comms for a in c.inputs])
 
@@ -230,10 +275,10 @@
         low, _, n, sums = blocks(rows, cols, steps)
 
         def compute(ins, outs):
-            g = (ins[0][...] + ins[1][...].astype(F32)).astype(BF16)
-            outs[0][...] = g
+            g = (ins[0][ALL] + ins[1][ALL].astype(F32)).astype(BF16)
+            outs[0][ALL] = g
             wide = g.astype(F32)
-            outs[1][...] = jnp.sum((wide * wide).reshape(-1, 8, wide.shape[1]), 0)
+            outs[1][ALL] = jnp.sum((wide * wide).reshape(-1, 8, wide.shape[1]), 0)
 
         return [(keep, low), (got, low)], [(shape(rows, cols), low), (shape(8 * n, cols, F32), sums)], compute
 
@@ -266,9 +311,9 @@
 
     def compute(step, ins, outs, scratch):
         choose(step, scratch[0])
-        a = norm_rows(ins[0][...].astype(F32))[1]
-        outs[0][...] = a
-        outs[1][...] = dot(a, scratch[0][...], 1, 0).astype(BF16)
+        a = norm_rows(ins[0][ALL].astype(F32))[1]
+        outs[0][ALL] = a
+        outs[1][ALL] = dot(a, scratch[0][ALL], 1, 0).astype(BF16)
 
     return run(number, 4, compute, [(h, block)], [(shape(tokens, d), block)] * 2, comms, [pltpu.VMEM((d, d), BF16)])
 
@@ -278,7 +323,7 @@
     m, n = tokens // 2, ff // 4
 
     def compute(step, ins, outs, _):
-        outs[0][...] = dot(ins[0][...], ins[1][...], 1, 0)
+        outs[0][ALL] = dot(ins[0][ALL], ins[1][ALL], 1, 0)
 
     return run(
         number, 8, compute,
@@ -294,9 +339,9 @@
     tile = pl.BlockSpec((m, n), lambda i: (i // 4, i % 4))
 
     def compute(step, ins, outs, _):
-        up = dot(ins[0][...], ins[1][...], 1, 0)
-        outs[0][...] = up
-        outs[1][...] = (jax.nn.silu(ins[2][...]) * up).astype(BF16)
+        up = dot(ins[0][ALL], ins[1][ALL], 1, 0)
+        outs[0][ALL] = up
+        outs[1][ALL] = (jax.nn.silu(ins[2][ALL]) * up).astype(BF16)
 
     return run(
         number, 8, compute,
@@ -312,19 +357,30 @@
     rows = pl.BlockSpec((m, d), lambda i: (i, 0))
 
     def compute(step, ins, outs, scratch):
+        held, sem = scratch[1:]
+
+        @pl.when(step == 0)
+        def _():
+            pltpu.make_async_copy(ins[1], held, sem).start()
+
         choose(step, scratch[0])
-        new = ins[2][...] + dot(ins[0][...], ins[1][...], 1, 0).astype(BF16)
+
+        @pl.when(step == 0)
+        def _():
+            pltpu.make_async_copy(ins[1], held, sem).wait()
+
+        new = ins[2][ALL] + dot(ins[0][ALL], held[ALL], 1, 0).astype(BF16)
         a = norm_rows(new.astype(F32))[1]
-        outs[0][...] = new
-        outs[1][...] = a
-        outs[2][...] = dot(a, scratch[0][...], 1, 0).astype(BF16)
+        outs[0][ALL] = new
+        outs[1][ALL] = a
+        outs[2][ALL] = dot(a, scratch[0][ALL], 1, 0).astype(BF16)
 
     return run(
         number, 4, compute,
-        [(s, pl.BlockSpec((m, ff), lambda i: (i, 0))), (w, pl.BlockSpec((ff, d), lambda i: (0, 0), pipeline_mode=pl.Buffered(1))), (h, rows)],
+        [(s, pl.BlockSpec((m, ff), lambda i: (i, 0))), (w, ANY), (h, rows)],
         [(shape(tokens, d), rows)] * 3,
         comms,
-        [pltpu.VMEM((d, d), BF16)],
+        [pltpu.VMEM((d, d), BF16), pltpu.VMEM((ff, d), BF16), pltpu.SemaphoreType.DMA],
     )
 
 
@@ -371,7 +427,7 @@
             outs[1][:rows, :] = self
             outs[1][rows:, :] = far
 
-        exchange(step, 4, lambda: dot(ins[0][...], ins[1][...], 0, 0), scratch, write)
+        exchange(step, 4, lambda: dot(ins[0][ALL], ins[1][ALL], 0, 0), scratch, write)
 
     return run(
         number, 8, compute,
@@ -406,7 +462,7 @@
             else:
                 send[rows:, :] = total.astype(BF16)
 
-        exchange(step, 4, lambda: dot(ins[0][...], ins[1][...], 0, 0), scratch, write)
+        exchange(step, 4, lambda: dot(ins[0][ALL], ins[1][ALL], 0, 0), scratch, write)
 
     return run(
         number, 8, compute,
@@ -424,12 +480,12 @@
     tile = pl.BlockSpec((m, n), lambda i: (i // 4, i % 4))
 
     def compute(step, ins, outs, _):
-        ds = dot(ins[0][...], ins[1][...], 1, 1).astype(BF16).astype(F32)
-        g, u = ins[2][...], ins[3][...]
+        ds = dot(ins[0][ALL], ins[1][ALL], 1, 1).astype(BF16).astype(F32)
+        g, u = ins[2][ALL], ins[3][ALL]
         sig = jax.nn.sigmoid(g)
         acted = g * sig
-        outs[0][...] = (ds * u * (sig * (1 + (g - acted)))).astype(BF16)
-        outs[1][...] = (ds * acted).astype(BF16)
+        outs[0][ALL] = (ds * u * (sig * (1 + (g - acted)))).astype(BF16)
+        outs[1][ALL] = (ds * acted).astype(BF16)
 
     return run(
         number, 8, compute,
@@ -448,13 +504,13 @@
     matrix = pl.BlockSpec((d, ff), lambda i: (0, 0), pipeline_mode=pl.Buffered(1))
 
     def compute(step, ins, outs, _):
-        da = dot(ins[0][...], ins[1][...], 1, 1).astype(BF16)
-        da = (da + dot(ins[2][...], ins[3][...], 1, 1).astype(BF16)).astype(F32)
-        wide = ins[4][...].astype(F32)
+        da = dot(ins[0][ALL], ins[1][ALL], 1, 1).astype(BF16)
+        da = (da + dot(ins[2][ALL], ins[3][ALL], 1, 1).astype(BF16)).astype(F32)
+        wide = ins[4][ALL].astype(F32)
         scale, _ = norm_rows(wide)
         inner = jnp.sum(da * wide, -1, keepdims=True) / d
         dh = da * scale - wide * (scale * scale * scale * inner)
-        outs[0][...] = ins[5][...] + dh.astype(BF16)
+        outs[0][ALL] = ins[5][ALL] + dh.astype(BF16)
 
     return run(
         number, 8, compute,
@@ -465,14 +521,17 @@
     )
 
 
-def k_tail(number, u_send, u_keep, d_got, d_keep, g_got, g_keep, squares):
+def k_tail(number, u_send, u_keep, d_got, d_keep, g_got, g_keep, sums):
     (rows2, cols), (d_rows, d_cols) = u_keep.shape, d_keep.shape
     rows, half, quarter = rows2 // 2, cols // 2, cols // 4
     others = [(i // 4, i // 2 % 2, i % 2) for i in range(1, 8)]
 
     def kernel(*refs):
-        u_s, u_k, d_g, d_k, g_g, g_k, sq_in, u_out, d_out, g_out, sq_out = refs[:11]
-        uk, uc, u2, uc2, dk, dc, gk, gg, g2, gc, slots, mine, local, send, receive = refs[11:]
+        refs = list(refs)
+        u_s, u_k, d_g, d_k, g_g, g_k = refs[:6]
+        so_far, refs = refs[6 : 6 + len(sums)], refs[6 + len(sums) :]
+        u_out, d_out, g_out, sq_out = refs[:4]
+        uk, uc, u2, uc2, dk, dc, gk, gg, g2, gc, slots, mine, local, send, receive = refs[4:]
         barrier = pltpu.get_barrier_semaphore()
         for flip in others:
             pl.semaphore_signal(barrier, inc=1, device_id={"dp": place(flip)}, device_id_type=MESH)
@@ -495,7 +554,7 @@
             one.start()
         loads[0].wait()
         loads[1].wait()
-        g2[...] = (gk[rows:, :] + gg[rows:, :].astype(F32)).astype(BF16)
+        g2[ALL] = (gk[rows:, :] + gg[rows:, :].astype(F32)).astype(BF16)
         gk[:rows, :] = gk[:rows, :] + gg[:rows, :].astype(F32)
         for one in g_hop:
             one.start()
@@ -507,14 +566,17 @@
             uk[:rows, at] = uk[:rows, at] + uc[:rows, at].astype(F32)
             second[i].start()
 
-        total = sq_in[...]
+        def folded(wide):
+            wide = jnp.sum(wide.reshape(-1, 8, wide.shape[1]), 0)
+            return sum(wide[:, k : k + 128] for k in range(0, wide.shape[1], 128))
+
+        total = sum(folded(one[ALL]) for one in so_far)
 
         def final(out, keep, came, at):
             g = (keep[: came.shape[0], at] + came[:, at].astype(F32)).astype(BF16)
             out[:, at] = g
             wide = g.astype(F32)
-            wide = jnp.sum((wide * wide).reshape(-1, 8, wide.shape[1]), 0)
-            return sum(wide[:, k : k + 128] for k in range(0, wide.shape[1], 128))
+            return folded(wide * wide)
 
         loads[3].wait()
         loads[4].wait()
@@ -525,7 +587,7 @@
         for i in (0, 2, 1, 3):
             second[i].wait_recv()
             total += final(u_out, uk, uc2, pl.ds(i * quarter, quarter))
-        mine[...] = total
+        mine[ALL] = total
         me = place((0, 0, 0))
         spread = [copy(10 + i, mine, slots.at[me], flip) for i, flip in enumerate(others)]
         for one in spread:
@@ -533,14 +595,14 @@
         slots[me] = total
         for one in spread:
             one.wait_recv()
-        sq_out[...] = sum(slots[i] for i in range(8))
+        sq_out[ALL] = sum(slots[i] for i in range(8))
         for one in first + g_hop + second + spread:
             one.wait_send()
 
     vmem = pl.BlockSpec(memory_space=pltpu.VMEM)
     return pl.pallas_call(
         kernel,
-        in_specs=[ANY] * 6 + [vmem],
+        in_specs=[ANY] * 6 + [vmem] * len(sums),
         out_specs=[vmem] * 4,
         out_shape=[shape(rows, cols), shape(d_rows, d_cols), shape(rows, cols), shape(8, 128, F32)],
         scratch_shapes=[
@@ -551,9 +613,9 @@
             pltpu.SemaphoreType.DMA((5,)), pltpu.SemaphoreType.DMA((17,)), pltpu.SemaphoreType.DMA((17,)),
         ],
         compiler_params=pltpu.CompilerParams(collective_id=number, has_side_effects=True, vmem_limit_bytes=VMEM_LIMIT),
-        cost_estimate=pl.CostEstimate(flops=10**9, bytes_accessed=5 * 10**7, transcendentals=0),
+        cost_estimate=COST,
         name=f"k{number}",
-    )(u_send, u_keep, d_got, d_keep, g_got, g_keep, squares)
+    )(u_send, u_keep, d_got, d_keep, g_got, g_keep, *sums)
 
 
 def adamw(w, m, v, g):
@@ -567,34 +629,30 @@
     def step(x, dy, *arrays):
         weights, ms, vs = (arrays[i : i + 3] for i in (0, 3, 6))
         h0, dy = x[0], dy[0]
-        (g0, g1), (u0, u1), (d0, d1) = ((w[0], w[1]) for w in weights)
-
-        a0, a0s, wg0 = k_norm(0, h0, [Gather(g0, 1)])
-        gate0, wu0 = k_gate(1, a0, wg0, [Gather(u0, 4)])
-        up0, s0, wd0 = k_up(2, a0, wu0, gate0, [Gather(d0, 4)])
-        h1, a1, a1s, wg1 = k_down(3, s0, wd0, h0, [Gather(g1, 2)])
-        gate1, wu1 = k_gate(4, a1, wg1, [Gather(u1, 4)])
-        up1, s1, wd1 = k_up(5, a1, wu1, gate1, [Gather(d1, 4)])
-
-        done, total = {}, 0.0
-        d1_send, d1_keep = k_gradient_down(6, s1, dy, [])
+        gate, up, down = weights
+
+        a0, a0s, wg0 = k_norm(0, h0, [Gather(gate, 0, 1)])
+        gate0, wu0 = k_gate(1, a0, wg0, [Gather(up, 0, 4)])
+        up0, s0, wd0 = k_up(2, a0, wu0, gate0, [Gather(down, 0, 4)])
+        h1, a1, a1s, wg1 = k_down(3, s0, wd0, h0, [Gather(gate, 1, 2)])
+        gate1, wu1 = k_gate(4, a1, wg1, [Gather(up, 1, 4)])
+        up1, s1, wd1 = k_up(5, a1, wu1, gate1, [Gather(down, 1, 4, rest=False)])
+
+        done = {}
+        d1_send, d1_keep, wd1 = k_gradient_down(6, s1, dy, [GatherRest(wd1, 6)])
         dgate1, dup1, got = k_back_gated(7, dy, wd1, gate1, up1, [Hop(d1_send, X, Y)])
         g1_send, g1_keep, d1_keep, got_d = k_gradient_in(8, a1s, dgate1, [AddHop(d1_keep, got, Y, X, 1)])
         u1_send, u1_keep, got = k_gradient_in(9, a1s, dup1, [Hop(g1_send, X, Y)])
-        dh1, done["d1"], sums, g1_keep, got_g, got = k_back_norm(
+        dh1, done["d1"], sums_d, g1_keep, got_g, got = k_back_norm(
             10, dgate1, wg1, dup1, wu1, h1, dy, [AddHop(g1_keep, got, Y, X, 1), Hop(u1_send, X, Y)], [side_last(d1_keep, got_d)]
         )
-        total += jnp.sum(sums)
-        d0_send, d0_keep, done["g1"], sums, u1_keep, got_u = k_gradient_down(
+        d0_send, d0_keep, done["g1"], sums_g, u1_keep, got_u = k_gradient_down(
             11, s0, dh1, [AddHop(u1_keep, got, Y, X, 1)], [side_last(g1_keep, got_g)]
         )
-        total += jnp.sum(sums)
-        dgate0, dup0, done["u1"], sums, got = k_back_gated(12, dh1, wd0, gate0, up0, [Hop(d0_send, X, Y)], [side_last(u1_keep, got_u)])
-        total += jnp.sum(sums)
+        dgate0, dup0, done["u1"], sums_u, got = k_back_gated(12, dh1, wd0, gate0, up0, [Hop(d0_send, X, Y)], [side_last(u1_keep, got_u)])
         g0_send, g0_keep, d0_keep, got_d = k_gradient_in(13, a0s, dgate0, [AddHop(d0_keep, got, Y, X, 1)])
         u0_send, u0_keep, got = k_gradient_in(14, a0s, dup0, [Hop(g0_send, X, Y)])
-        squares = jnp.zeros((8, 128), F32).at[0, 0].set(total)
-        done["u0"], done["d0"], done["g0"], squares = k_tail(15, u0_send, u0_keep, got_d, d0_keep, got, g0_keep, squares)
+        done["u0"], done["d0"], done["g0"], squares = k_tail(15, u0_send, u0_keep, got_d, d0_keep, got, g0_keep, (sums_d, sums_g, sums_u))
         total = jnp.sum(squares)
         count = 8 * sum(g.size for g in done.values())
         factor = jnp.minimum(1.0, 0.5 * lax.rsqrt(total / count + 1e-30))

time: 974 us -> 941 us (0.966)
  Pallas kernels: 912 us -> 895 us
    pallas_call x16, Pallas kernels: 912 us -> 895 us  [the longest x15 814 us: run(): pl.pallas_call(kernel, grid=(steps,), input_output_aliases=aliases, in_sp...]
where the time goes in v3:
time: 941 us; the launch traced here: 935 us
  Pallas kernels  895 us (95%)
  other arithmetic  35.6 us (4%)
    pallas_call x15, Pallas kernels, run(): pl.pallas_call(kernel, grid=(steps,), input_output_aliases=aliases, in_sp...  814 us
    pallas_call x1, Pallas kernels, k_tail(): pl.pallas_call(kernel, in_specs=[ANY] * 6 + [vmem] * len(sums), out_specs...  80.8 us
    convert_element_type x2, other arithmetic, adamw(): return ((w - 0.02 * step).astype(BF16), m, v)  34.3 us

profile of v3, /device:TPU:0, one launch (start us, length us, event | category | flops | bytes accessed | tf_op | source)
XLA Modules:
  0.0 934.5 jit_solution(4169394674172458511)
XLA Ops:
  0.6 63.1 %k0.1 = (bf16[2048,1280]{1,0:T(8,128)(2,1)}, bf16[2048,1280]{1,0:T(8,128)(2,1)}, bf16[1280,5120]{1,0:T(8,128)(2,1)}) custom-call(bf16[2048,1280]{1,0:T(8,128)(2,1)} %bitcast.20, bf16[320,5120]{1,0:T(8,128)(2,1)} %bitcast.16), custom_call_target="tpu_custom_call" | custom-call | flops 1000000000 | bytes 50000000 | tf_op jit(solution)/shard_map/k0/pallas_call | solution.py:247
  63.8 63.0 %k1.1 = (f32[2048,5120]{1,0:T(8,128)}, bf16[1280,5120]{1,0:T(8,128)(2,1)}) custom-call(bf16[2048,1280]{1,0:T(8,128)(2,1)} %get-tuple-element.68.refs_0_, bf16[1280,5120]{1,0:T(8,128)(2,1)} %get-tuple-element.69.refs_1_, bf16[320,5120]{1,0:T(8,128)(2,1)} %bitcast.14), custom_call_target="tpu_custom_call" | custom-call | flops 1000000000 | bytes 50000000 | tf_op jit(solution)/shard_map/k1/pallas_call | solution.py:247
  126.7 65.5 %k2.1 = (f32[2048,5120]{1,0:T(8,128)}, bf16[2048,5120]{1,0:T(8,128)(2,1)}, bf16[5120,1280]{1,0:T(8,128)(2,1)}) custom-call(bf16[2048,1280]{1,0:T(8,128)(2,1)} %get-tuple-element.68.refs_0_, bf16[1280,5120]{1,0:T(8,128)(2,1)} %get-tuple-element.70.refs_1_, f32[2048,5120]{1,0:T(8,128)} %get-tuple-element.71.refs_2_, bf16[1280,1280]{1,0:T(8,128)(2,1)} %bitcast.18), custom_call_target="tpu_custom_call" | custom-call | flops 1000000000 | bytes 50000000 | tf_op jit(solution)/shard_map/k2/pallas_call | solution.py:247
  192.2 62.8 %k3.1 = (bf16[2048,1280]{1,0:T(8,128)(2,1)}, bf16[2048,1280]{1,0:T(8,128)(2,1)}, bf16[2048,1280]{1,0:T(8,128)(2,1)}, bf16[1280,5120]{1,0:T(8,128)(2,1)}) custom-call(bf16[2048,5120]{1,0:T(8,128)(2,1)} %get-tuple-element.72.refs_0_, bf16[5120,1280]{1,0:T(8,128)(2,1)} %get-tuple-element.73.refs_1_, bf16[2048,1280]{1,0:T(8,128)(2,1)} %bitcast.21, ...), custom_call_target="tpu_custom_call" | custom-call | flops 1000000000 | bytes 50000000 | tf_op jit(solution)/shard_map/k3/pallas_call | solution.py:247
  255.1 63.0 %k4.1 = (f32[2048,5120]{1,0:T(8,128)}, bf16[1280,5120]{1,0:T(8,128)(2,1)}) custom-call(bf16[2048,1280]{1,0:T(8,128)(2,1)} %get-tuple-element.74.refs_0_, bf16[1280,5120]{1,0:T(8,128)(2,1)} %get-tuple-element.75.refs_1_, bf16[320,5120]{1,0:T(8,128)(2,1)} %bitcast.15), custom_call_target="tpu_custom_call" | custom-call | flops 1000000000 | bytes 50000000 | tf_op jit(solution)/shard_map/k4/pallas_call | solution.py:247
  318.1 58.3 %k5.1 = (f32[2048,5120]{1,0:T(8,128)}, bf16[2048,5120]{1,0:T(8,128)(2,1)}, bf16[5120,1280]{1,0:T(8,128)(2,1)}) custom-call(bf16[2048,1280]{1,0:T(8,128)(2,1)} %get-tuple-element.74.refs_0_, bf16[1280,5120]{1,0:T(8,128)(2,1)} %get-tuple-element.76.refs_1_.refs_3_, f32[2048,5120]{1,0:T(8,128)} %get-tuple-element.77.refs_2_, bf16[1280,1280]{1,0:T(8,128)(2,1)} %bitcast.19), custom_call_target="tpu_custom_call" | custom-call | flops 1000000000 | bytes 50000000 | tf_op jit(solution)/shard_map/k5/pallas_call | solution.py:247
  376.4 40.5 %k6.1 = (bf16[1280,1280]{1,0:T(8,128)(2,1)}, f32[1280,1280]{1,0:T(8,128)}, bf16[5120,1280]{1,0:T(8,128)(2,1)}) custom-call(bf16[2048,5120]{1,0:T(8,128)(2,1)} %get-tuple-element.78.refs_0_, bf16[2048,1280]{1,0:T(8,128)(2,1)} %bitcast.11, bf16[5120,1280]{1,0:T(8,128)(2,1)} %get-tuple-element.79.refs_2_), custom_call_target="tpu_custom_call", output_to_operand_aliasing={{2}: (2, {})} | custom-call | flops 1000000000 | bytes 50000000 | tf_op jit(solution)/shard_map/k6/pallas_call | solution.py:247
  416.9 59.0 %k7.1 = (bf16[2048,5120]{1,0:T(8,128)(2,1)}, bf16[2048,5120]{1,0:T(8,128)(2,1)}, bf16[1280,1280]{1,0:T(8,128)(2,1)}) custom-call(bf16[2048,1280]{1,0:T(8,128)(2,1)} %bitcast.12, bf16[5120,1280]{1,0:T(8,128)(2,1)} %get-tuple-element.80.refs_1_, f32[2048,5120]{1,0:T(8,128)} %get-tuple-element.77.refs_2_, f32[2048,5120]{1,0:T(8,128)} %get-tuple-element.81.refs_3_, ...), custom_call_target="tpu_custom_call" | custom-call | flops 1000000000 | bytes 50000000 | tf_op jit(solution)/shard_map/k7/pallas_call | solution.py:247
  475.9 38.4 %k8.1 = (bf16[320,5120]{1,0:T(8,128)(2,1)}, f32[320,5120]{1,0:T(8,128)}, f32[640,1280]{1,0:T(8,128)}, bf16[640,1280]{1,0:T(8,128)(2,1)}) custom-call(bf16[2048,1280]{1,0:T(8,128)(2,1)} %get-tuple-element.86.refs_0_, bf16[2048,5120]{1,0:T(8,128)(2,1)} %get-tuple-element.83.refs_1_.refs_0_, f32[1280,1280]{1,0:T(8,128)} %get-tuple-element.87.refs_2_, ...), custom_call_target="tpu_custom_call" | custom-call | flops 1000000000 | bytes 50000000 | tf_op jit(solution)/shard_map/k8/pallas_call | solution.py:247
  514.3 42.4 %k9.1 = (bf16[320,5120]{1,0:T(8,128)(2,1)}, f32[320,5120]{1,0:T(8,128)}, bf16[320,5120]{1,0:T(8,128)(2,1)}) custom-call(bf16[2048,1280]{1,0:T(8,128)(2,1)} %get-tuple-element.86.refs_0_, bf16[2048,5120]{1,0:T(8,128)(2,1)} %get-tuple-element.84.refs_1_.refs_2_, bf16[320,5120]{1,0:T(8,128)(2,1)} %get-tuple-element.92.refs_2_), custom_call_target="tpu_custom_call" | custom-call | flops 1000000000 | bytes 50000000 | tf_op jit(solution)/shard_map/k9/pallas_call | solution.py:247
  556.7 74.8 %k10.1 = (bf16[2048,1280]{1,0:T(8,128)(2,1)}, bf16[640,1280]{1,0:T(8,128)(2,1)}, f32[64,1280]{1,0:T(8,128)}, f32[160,5120]{1,0:T(8,128)}, bf16[160,5120]{1,0:T(8,128)(2,1)}, /*index=5*/bf16[320,5120]{1,0:T(8,128)(2,1)}) custom-call(bf16[2048,5120]{1,0:T(8,128)(2,1)} %get-tuple-element.83.refs_1_.refs_0_, bf16[1280,5120]{1,0:T(8,128)(2,1)} %get-tuple-element.75.refs_1_, ...), custom_call_target="tpu_custom_call" | custom-call | flops 1000000000 | bytes 50000000 | tf_op jit(solution)/shard_map/k10/pallas_call | solution.py:247
  631.5 42.0 %k11.1 = (bf16[1280,1280]{1,0:T(8,128)(2,1)}, f32[1280,1280]{1,0:T(8,128)}, bf16[160,5120]{1,0:T(8,128)(2,1)}, f32[8,5120]{1,0:T(8,128)}, f32[160,5120]{1,0:T(8,128)}, /*index=5*/bf16[160,5120]{1,0:T(8,128)(2,1)}) custom-call(bf16[2048,5120]{1,0:T(8,128)(2,1)} %get-tuple-element.72.refs_0_, bf16[2048,1280]{1,0:T(8,128)(2,1)} %get-tuple-element.95.refs_1_.refs_0_, ...), custom_call_target="tpu_custom_call" | custom-call | flops 1000000000 | bytes 50000000 | tf_op jit(solution)/shard_map/k11/pallas_call | solution.py:247
  673.6 60.7 %k12.1 = (bf16[2048,5120]{1,0:T(8,128)(2,1)}, bf16[2048,5120]{1,0:T(8,128)(2,1)}, bf16[160,5120]{1,0:T(8,128)(2,1)}, f32[8,5120]{1,0:T(8,128)}, bf16[1280,1280]{1,0:T(8,128)(2,1)}) custom-call(bf16[2048,1280]{1,0:T(8,128)(2,1)} %get-tuple-element.95.refs_1_.refs_0_, bf16[5120,1280]{1,0:T(8,128)(2,1)} %get-tuple-element.73.refs_1_, ...), custom_call_target="tpu_custom_call" | custom-call | flops 1000000000 | bytes 50000000 | tf_op jit(solution)/shard_map/k12/pallas_call | solution.py:247
  734.3 37.9 %k13.1 = (bf16[320,5120]{1,0:T(8,128)(2,1)}, f32[320,5120]{1,0:T(8,128)}, f32[640,1280]{1,0:T(8,128)}, bf16[640,1280]{1,0:T(8,128)(2,1)}) custom-call(bf16[2048,1280]{1,0:T(8,128)(2,1)} %get-tuple-element.67.refs_0_, bf16[2048,5120]{1,0:T(8,128)(2,1)} %get-tuple-element.105.refs_1_, f32[1280,1280]{1,0:T(8,128)} %get-tuple-element.106.refs_2_, ...), custom_call_target="tpu_custom_call" | custom-call | flops 1000000000 | bytes 50000000 | tf_op jit(solution)/shard_map/k13/pallas_call | solution.py:247
  772.1 42.7 %k14.1 = (bf16[320,5120]{1,0:T(8,128)(2,1)}, f32[320,5120]{1,0:T(8,128)}, bf16[320,5120]{1,0:T(8,128)(2,1)}) custom-call(bf16[2048,1280]{1,0:T(8,128)(2,1)} %get-tuple-element.67.refs_0_, bf16[2048,5120]{1,0:T(8,128)(2,1)} %get-tuple-element.104.refs_1_, bf16[320,5120]{1,0:T(8,128)(2,1)} %get-tuple-element.108.refs_2_), custom_call_target="tpu_custom_call" | custom-call | flops 1000000000 | bytes 50000000 | tf_op jit(solution)/shard_map/k14/pallas_call | solution.py:247
  814.8 80.8 %k15.1 = (bf16[160,5120]{1,0:T(8,128)(2,1)}, bf16[640,1280]{1,0:T(8,128)(2,1)}, bf16[160,5120]{1,0:T(8,128)(2,1)}, f32[8,128]{1,0:T(8,128)}) custom-call(bf16[320,5120]{1,0:T(8,128)(2,1)} %get-tuple-element.109.refs_0_, f32[320,5120]{1,0:T(8,128)} %get-tuple-element.110.refs_1_, bf16[640,1280]{1,0:T(8,128)(2,1)} %get-tuple-element.111.refs_2_, ...), custom_call_target="tpu_custom_call" | custom-call | flops 1000000000 | bytes 50000000 | tf_op jit(solution)/shard_map/k15/pallas_call | solution.py:603
  895.6 1.3 reduce_sum.9
  897.6 0.0 copy-start
  897.6 0.0 copy-start.1
  897.6 0.0 copy-start.2
  897.6 0.0 copy-start.3
  897.6 0.0 copy-start.4
  897.6 0.0 copy-start.5
  897.7 13.9 %fusion.8 = (bf16[2,640,1280]{2,1,0:T(8,128)(2,1)}, f32[2,640,1280]{2,1,0:T(8,128)}, f32[2,640,1280]{2,1,0:T(8,128)}) fusion(bf16[2,640,1280]{2,1,0:T(8,128)(2,1)} %param.15, f32[]{:T(128)S(6)} %min_shard_map.3, bf16[1,640,1280]{2,1,0:T(8,128)(2,1)} %bitcast.22, bf16[1,640,1280]{2,1,0:T(8,128)(2,1)} %bitcast.27, f32[2,640,1280]{2,1,0:T(8,128)} %param.21, ...), kind=kLoop, calls=%fused_computation.17 | loop fusion | flops 32768000 | bytes 36044804 | tf_op jit(solution)/shard_map/convert_element_type | solution.py:625
  911.6 0.0 copy-done
  911.6 0.0 copy-done.1
  911.6 0.0 copy-done.2
  911.6 1.1 copy-done.3
  912.7 0.5 copy-done.4
  913.2 0.5 copy-done.5
  913.7 20.4 %fusion.2 = (bf16[2,160,5120]{2,1,0:T(8,128)(2,1)}, f32[2,160,5120]{2,1,0:T(8,128)}, f32[2,160,5120]{2,1,0:T(8,128)}, bf16[2,160,5120]{2,1,0:T(8,128)(2,1)}, f32...) fusion(bf16[2,160,5120]{2,1,0:T(8,128)(2,1)S(1)} %copy-done.1, f32[]{:T(128)S(6)} %min_shard_map.3, ...), kind=kLoop, calls=%fused_computation.11 | loop fusion | flops 65536000 | bytes 72089600 | tf_op jit(solution)/shard_map/convert_element_type | solution.py:625
Async XLA Ops:
  897.6 14.0 %copy-start = (bf16[2,160,5120]{2,1,0:T(8,128)(2,1)S(1)}, bf16[2,160,5120]{2,1,0:T(8,128)(2,1)}, u32[]{:S(2)}) copy-start(bf16[2,160,5120]{2,1,0:T(8,128)(2,1)} %param.14) | copy-start | bytes 9830404
  897.6 14.0 %copy-start.1 = (bf16[2,160,5120]{2,1,0:T(8,128)(2,1)S(1)}, bf16[2,160,5120]{2,1,0:T(8,128)(2,1)}, u32[]{:S(2)}) copy-start(bf16[2,160,5120]{2,1,0:T(8,128)(2,1)} %param.13) | copy-start | bytes 9830404
  897.6 14.0 %copy-start.2 = (bf16[160,5120]{1,0:T(8,128)(2,1)S(1)}, bf16[160,5120]{1,0:T(8,128)(2,1)}, u32[]{:S(2)}) copy-start(bf16[160,5120]{1,0:T(8,128)(2,1)} %get-tuple-element.119) | copy-start | bytes 4915204
  897.6 15.1 %copy-start.3 = (bf16[160,5120]{1,0:T(8,128)(2,1)S(1)}, bf16[160,5120]{1,0:T(8,128)(2,1)}, u32[]{:S(2)}) copy-start(bf16[160,5120]{1,0:T(8,128)(2,1)} %get-tuple-element.122) | copy-start | bytes 4915204
  897.6 15.5 %copy-start.4 = (bf16[160,5120]{1,0:T(8,128)(2,1)S(1)}, bf16[160,5120]{1,0:T(8,128)(2,1)}, u32[]{:S(2)}) copy-start(bf16[160,5120]{1,0:T(8,128)(2,1)} %get-tuple-element.121) | copy-start | bytes 4915204
  897.6 16.0 %copy-start.5 = (bf16[160,5120]{1,0:T(8,128)(2,1)S(1)}, bf16[160,5120]{1,0:T(8,128)(2,1)}, u32[]{:S(2)}) copy-start(bf16[160,5120]{1,0:T(8,128)(2,1)} %get-tuple-element.118) | copy-start | bytes 4915204
